TPU v7x, 256 devices: a whole 4x4x8 slice. The times are simulated.
256 devices in a mesh: row: 16 (over x_lo, y, core), col: 16 (over z, x_hi).
Axes of the slice: x: 4 (x_hi: 2, x_lo: 2; x = x_hi * 2 + x_lo), y: 4, z: 8, core: 2. Of those that a mesh axis runs over, the one named last changes fastest.
Arguments:
- labels: int32 [16, 512, 2048], P(None, 'row', 'col'), may hold values from 0 to 11
- pressure: float32 [16, 512, 2048], P(None, 'row', 'col'), may hold values from -6 to 6
- velocity_x: float32 [16, 512, 2048], P(None, 'row', 'col'), may hold values from -6 to 6
- velocity_y: float32 [16, 512, 2048], P(None, 'row', 'col'), may hold values from -6 to 6
- velocity_z: float32 [16, 512, 2048], P(None, 'row', 'col'), may hold values from -6 to 6
- speed_table: float32 [12], replicated, may hold values from 0.8 to 2
- density_table: float32 [12], replicated, may hold values from 0.9 to 1.9
- filter_taps: float32 [33], replicated, may hold values from -0.2 to 0.8, as said below
- layer_width: int32 [4], replicated, may hold values from 10 to 40
Outputs:
- pressure_next: float32 [16, 512, 2048], P(None, 'row', 'col')
- velocity_x_next: float32 [16, 512, 2048], P(None, 'row', 'col')
- velocity_y_next: float32 [16, 512, 2048], P(None, 'row', 'col')
- velocity_z_next: float32 [16, 512, 2048], P(None, 'row', 'col')
Inputs may be any that keep to these rules, and one draw needn't show every extreme that they name: `filter_taps`: tap k weighs the cell k - 16 positions away.
All inputs are finite; a program needn't handle non-finite values.
Results may differ from a plain program's by a relative error of at most 0.000068.
Values sent between devices are 32-bit elements; how exact they have to be, the bound alone decides.
A program may use at most 64 MiB of HBM per device.

v0:
```python
import math

import jax
import jax.numpy as jnp
from jax import lax
from jax.sharding import PartitionSpec as P

time_step = 0.15
reference_speed = 2.0
absorption = 6.0
highest = lax.Precision.HIGHEST


def extended(array, sides, width):
    for axis, dim in sides:
        size, length = (lax.axis_size(axis), array.shape[dim])
        up = [(i, (i + 1) % size) for i in range(size)]
        down = [(j, i) for i, j in up]
        last = lax.slice_in_dim(array, length - width, length, axis=dim)
        initial = lax.slice_in_dim(array, 0, width, axis=dim)
        before = lax.ppermute(last, axis, up)
        after = lax.ppermute(initial, axis, down)
        array = jnp.concatenate([before, array, after], axis=dim)
    return array


def factor_pair(length):
    leading = math.gcd(length, 2 ** ((length.bit_length() - 1) // 2))
    return (leading, length // leading)


def angle_table(height, breadth, length, phase_sign):
    product = (
        jnp.arange(height, dtype=jnp.int32)[:, None]
        * jnp.arange(breadth, dtype=jnp.int32)[None, :]
        % length
    )
    angles = product.astype(jnp.float32) * (2.0 * math.pi / length)
    return (jnp.cos(angles), phase_sign * jnp.sin(angles))


def complex_contract(pieces, tables, form):
    real_part, imag_part = pieces
    cosines, sine_part = tables

    def product(operand, matrix):
        return jnp.einsum(form, operand, matrix, precision=highest)

    return (
        product(real_part, cosines) - product(imag_part, sine_part),
        product(real_part, sine_part) + product(imag_part, cosines),
    )


def complex_times(factor, pieces):
    return (
        factor[0] * pieces[0] - factor[1] * pieces[1],
        factor[0] * pieces[1] + factor[1] * pieces[0],
    )


def line_transform(pieces, on_last, inverse):
    real_part, imag_part = pieces
    position = real_part.ndim - 1 if on_last else real_part.ndim - 2
    length = real_part.shape[position]
    leading, trailing = factor_pair(length)
    phase_sign = 1.0 if inverse else -1.0
    new_shape = real_part.shape[:position] + (leading, trailing) + real_part.shape[position + 1 :]
    pieces = (real_part.reshape(new_shape), imag_part.reshape(new_shape))
    outer_table = angle_table(leading, leading, leading, phase_sign)
    inner_table = angle_table(trailing, trailing, trailing, phase_sign)
    twiddle = angle_table(leading, trailing, length, phase_sign)
    suffix = ""
    if not on_last:
        twiddle = (twiddle[0][:, :, None], twiddle[1][:, :, None])
        suffix = "x"
    if inverse:
        pieces = complex_contract(pieces, inner_table, "...kl" + suffix + ",lb->...kb" + suffix)
        pieces = complex_times(twiddle, pieces)
        pieces = complex_contract(pieces, outer_table, "...kb" + suffix + ",ka->...ab" + suffix)
        factor = 1.0 / length
        pieces = (pieces[0] * factor, pieces[1] * factor)
    else:
        pieces = complex_contract(pieces, outer_table, "...ab" + suffix + ",ak->...kb" + suffix)
        pieces = complex_times(twiddle, pieces)
        pieces = complex_contract(pieces, inner_table, "...kb" + suffix + ",bl->...kl" + suffix)
    initial = real_part.shape
    return (pieces[0].reshape(initial), pieces[1].reshape(initial))


def transform_x(pieces):
    return line_transform(pieces, True, False)


def transform_y(pieces):
    return line_transform(pieces, False, False)


def untransform_x(pieces):
    return line_transform(pieces, True, True)


def untransform_y(pieces):
    return line_transform(pieces, False, True)


def depth_forward(pieces):
    length = pieces[0].shape[1]
    return complex_contract(pieces, angle_table(length, length, length, -1.0), "fzyx,zk->fkyx")


def depth_inverse(pieces):
    length = pieces[0].shape[1]
    result = complex_contract(pieces, angle_table(length, length, length, 1.0), "fkyx,kz->fzyx")
    factor = 1.0 / length
    return (result[0] * factor, result[1] * factor)


def packed(operation, stacked):
    result = operation((stacked[0], stacked[1]))
    return jnp.stack([result[0], result[1]])


def natural_wave(indices, length):
    signed = jnp.where(indices < length // 2, indices, indices - length)
    return signed.astype(jnp.float32) * (2.0 * math.pi / length)


def ordered_wave(position, length):
    leading, trailing = factor_pair(length)
    return natural_wave(position // trailing + leading * (position % trailing), length)


def forward_rows(pieces):
    pieces = depth_forward(pieces)
    stacked = jnp.stack([pieces[0], pieces[1]])
    stacked = packed(
        transform_y, lax.all_to_all(stacked, "row", split_axis=2, concat_axis=3, tiled=True)
    )
    stacked = packed(
        transform_x, lax.all_to_all(stacked, "col", split_axis=3, concat_axis=4, tiled=True)
    )
    return (stacked[0], stacked[1])


def inverse_rows(pieces):
    pieces = untransform_x(pieces)
    stacked = jnp.stack([pieces[0], pieces[1]])
    stacked = packed(
        untransform_y, lax.all_to_all(stacked, "col", split_axis=4, concat_axis=3, tiled=True)
    )
    stacked = packed(
        depth_inverse, lax.all_to_all(stacked, "row", split_axis=3, concat_axis=2, tiled=True)
    )
    return (stacked[0], stacked[1])


def waves_rows(spectral_shape):
    planes, height, breadth = (spectral_shape[1], spectral_shape[2], spectral_shape[3])
    depth_ids = lax.axis_index("row") * planes + jnp.arange(planes, dtype=jnp.int32)
    cross_ids = lax.axis_index("col") * height + jnp.arange(height, dtype=jnp.int32)
    wave_z = natural_wave(depth_ids, planes * lax.axis_size("row"))[:, None, None]
    wave_y = ordered_wave(cross_ids, height * lax.axis_size("col"))[None, :, None]
    wave_x = ordered_wave(jnp.arange(breadth, dtype=jnp.int32), breadth)[None, None, :]
    return (wave_z, wave_y, wave_x)


def derivative(wavenum, correction, phase_sign):
    half_wave = 0.5 * wavenum
    return (
        phase_sign * wavenum * jnp.sin(half_wave) * correction,
        wavenum * jnp.cos(half_wave) * correction,
    )


def band_matrix(filter_taps, extent):
    tap_count = filter_taps.shape[0]
    offset = (
        jnp.arange(extent + tap_count - 1, dtype=jnp.int32)[:, None]
        - jnp.arange(extent, dtype=jnp.int32)[None, :]
    )
    selected = offset[:, :, None] == jnp.arange(tap_count, dtype=jnp.int32)[None, None, :]
    return jnp.sum(jnp.where(selected, filter_taps[None, None, :], 0.0), axis=2)


def absorber(position, length, low_width, high_width):
    low_part = jnp.maximum(low_width - position, 0).astype(jnp.float32) / low_width.astype(
        jnp.float32
    )
    high_part = jnp.maximum(position - (length - 1 - high_width), 0).astype(
        jnp.float32
    ) / high_width.astype(jnp.float32)
    damping = absorption * reference_speed * (low_part**4 + high_part**4)
    return jnp.exp(-0.5 * time_step * damping)


def spectral_correction(wave_z, wave_y, wave_x):
    return jnp.sinc(
        reference_speed
        * time_step
        * jnp.sqrt(wave_x * wave_x + wave_y * wave_y + wave_z * wave_z)
        / (2.0 * math.pi)
    )


def on_device(
    labels,
    pressure,
    velocity_x,
    velocity_y,
    velocity_z,
    speed_table,
    density_table,
    filter_taps,
    layer_width,
):
    planes, height, breadth = pressure.shape
    buoyancy_of = 1.0 / density_table
    modulus_of = density_table * speed_table * speed_table
    buoyancy = jnp.zeros(pressure.shape, jnp.float32)
    modulus = jnp.zeros(pressure.shape, jnp.float32)
    for label_id in range(speed_table.shape[0]):
        matches = labels == label_id
        buoyancy = jnp.where(matches, buoyancy_of[label_id], buoyancy)
        modulus = jnp.where(matches, modulus_of[label_id], modulus)
    coefficients = jnp.stack([buoyancy, modulus])
    reach = filter_taps.shape[0] // 2
    across = band_matrix(filter_taps, breadth)
    downward = band_matrix(filter_taps, height)
    padded = extended(coefficients, (("col", 3),), reach)
    smoothed = jnp.einsum("fzyj,ji->fzyi", padded, across, precision=highest)
    padded = extended(smoothed, (("row", 2),), reach)
    smoothed = jnp.einsum("fzjx,jy->fzyx", padded, downward, precision=highest)
    buoyancy = smoothed[0]
    modulus = smoothed[1]
    column_ids = lax.axis_index("col") * breadth + jnp.arange(breadth, dtype=jnp.int32)
    row_ids = lax.axis_index("row") * height + jnp.arange(height, dtype=jnp.int32)
    damp_x = absorber(column_ids, breadth * lax.axis_size("col"), layer_width[0], layer_width[1])[
        None, None, :
    ]
    damp_y = absorber(row_ids, height * lax.axis_size("row"), layer_width[2], layer_width[3])[
        None, :, None
    ]
    empty = jnp.zeros(pressure.shape, jnp.float32)
    forward, inverse, waves_of = (forward_rows, inverse_rows, waves_rows)
    pressure_hat = forward((pressure[None], empty[None]))
    wave_z, wave_y, wave_x = waves_of(pressure_hat[0].shape)
    correction = spectral_correction(wave_z, wave_y, wave_x)
    pressure_one = (pressure_hat[0][0], pressure_hat[1][0])
    grad_x_hat = complex_times(derivative(wave_x, correction, -1.0), pressure_one)
    grad_y_hat = complex_times(derivative(wave_y, correction, -1.0), pressure_one)
    grad_z_hat = complex_times(derivative(wave_z, correction, -1.0), pressure_one)
    packed_real = jnp.stack([grad_x_hat[0] - grad_y_hat[1], grad_z_hat[0]])
    packed_imag = jnp.stack([grad_x_hat[1] + grad_y_hat[0], grad_z_hat[1]])
    gradients = inverse((packed_real, packed_imag))
    grad_x = gradients[0][0]
    grad_y = gradients[1][0]
    grad_z = gradients[0][1]
    next_x = damp_x * (damp_x * velocity_x - time_step * buoyancy * grad_x)
    next_y = damp_y * (damp_y * velocity_y - time_step * buoyancy * grad_y)
    next_z = velocity_z - time_step * buoyancy * grad_z
    velocity_hat = forward((jnp.stack([next_x, next_z]), jnp.stack([next_y, empty])))
    horizontal = (velocity_hat[0][0], velocity_hat[1][0])
    vertical = (velocity_hat[0][1], velocity_hat[1][1])
    flow_x = complex_times(derivative(wave_x, correction, 1.0), horizontal)
    flow_y = complex_times(derivative(wave_y, correction, 1.0), horizontal)
    flow_z = complex_times(derivative(wave_z, correction, 1.0), vertical)
    summed_real = flow_x[0] + flow_y[1] + flow_z[0]
    summed_imag = flow_x[1] - flow_y[0] + flow_z[1]
    divergence = inverse((summed_real[None], summed_imag[None]))[0][0]
    damp_both = damp_x * damp_y
    pressure_next = damp_both * (damp_both * pressure - time_step * modulus * divergence)
    return (pressure_next, next_x, next_y, next_z)


def solution(mesh):
    return jax.shard_map(
        on_device,
        mesh=mesh,
        in_specs=(
            P(None, "row", "col"),
            P(None, "row", "col"),
            P(None, "row", "col"),
            P(None, "row", "col"),
            P(None, "row", "col"),
            P(),
            P(),
            P(),
            P(),
        ),
        out_specs=(
            P(None, "row", "col"),
            P(None, "row", "col"),
            P(None, "row", "col"),
            P(None, "row", "col"),
        ),
        check_vma=False,
    )
```

profile of v0, /device:TPU:1, one launch (start us, length us, event | category | flops | bytes accessed | tf_op | source)
XLA Modules:
  0.0 320.3 jit_solution(11069281004676494393)
XLA Ops:
  5.2 6.9 %all-to-all-start = ((f32[2,1,16,32,128]{4,3,1,0,2:T(8,128)}), f32[2,1,16,32,128]{4,3,1,0,2:T(8,128)S(1)}, u32[]{:S(2)}, u32[]{:S(2)}) async-start(f32[2,1,16,32,128]{4,3,1,0,2:T(8,128)} %copy.316), calls=%async_computation | async-start | bytes 1048576 | tf_op jit(solution)/shard_map/all_to_all | solution.py:138
  12.4 9.4 %all-to-all-done = f32[2,1,16,32,128]{4,3,1,0,2:T(8,128)S(1)} async-done(((f32[2,1,16,32,128]{4,3,1,0,2:T(8,128)}), f32[2,1,16,32,128]{4,3,1,0,2:T(8,128)S(1)}, u32[]{:S(2)}, u32[]{:S(2)}) %all-to-all-start) | async-done | bytes 524320 | tf_op jit(solution)/shard_map/all_to_all | solution.py:138
  27.1 10.6 %all-to-all-start.1 = ((f32[2,1,1,512,128]{4,2,1,0,3:T(1,128)}), f32[2,1,1,512,128]{4,2,1,0,3:T(1,128)S(1)}, u32[]{:S(2)}, u32[]{:S(2)}) async-start(f32[2,1,1,512,128]{4,2,1,0,3:T(1,128)} %pad_maximum_fusion.6), calls=%async_computation.1 | async-start | bytes 1048576 | tf_op jit(solution)/shard_map/all_to_all | solution.py:141
  39.0 15.4 %all-to-all-done.1 = f32[2,1,1,512,128]{4,2,1,0,3:T(1,128)S(1)} async-done(((f32[2,1,1,512,128]{4,2,1,0,3:T(1,128)}), f32[2,1,1,512,128]{4,2,1,0,3:T(1,128)S(1)}, u32[]{:S(2)}, u32[]{:S(2)}) %all-to-all-start.1) | async-done | bytes 524320 | tf_op jit(solution)/shard_map/all_to_all | solution.py:141
  70.8 3.9 %copy.390 = f32[2,1,32,32,64]{2,0,4,3,1:T(2,128)} copy(f32[2,1,32,32,64]{4,3,2,0,1:T(8,128)} %fusion.5) | data formatting | bytes 1048576 | tf_op jit(solution)/shard_map/stack;reshape | solution.py:148
  76.8 4.1 %copy.391 = f32[2,1,32,32,64]{2,0,4,3,1:T(2,128)} copy(f32[2,1,32,32,64]{4,3,2,0,1:T(8,128)} %fusion.3) | data formatting | bytes 1048576 | tf_op jit(solution)/shard_map/stack;reshape | solution.py:148
  80.9 5.2 %fusion.760 = f32[2048,2,1,2,32]{4,3,2,1,0:T(2,128)} fusion(f32[1,2,1,32,2048]{3,1,2,0,4:T(2,128)} %bitcast.572, f32[1,2,1,32,2048]{3,1,2,0,4:T(2,128)S(1)} %bitcast.571), kind=kLoop, calls=%fused_computation.852 | loop fusion | flops 262144 | bytes 2097152
  86.1 6.6 %reshape.1299 = f32[16,1,16384]{2,1,0:T(1,128)} reshape(f32[2048,2,1,2,32]{4,3,2,1,0:T(2,128)} %fusion.760) | data formatting | bytes 2097152
  92.7 4.5 %all-to-all-start.2 = ((f32[16,1,16384]{2,1,0:T(1,128)}), f32[16,1,16384]{2,1,0:T(1,128)S(1)}, u32[]{:S(2)}, u32[]{:S(2)}) async-start(f32[16,1,16384]{2,1,0:T(1,128)} %reshape.1299), calls=%async_computation.2 | async-start | bytes 2097152 | tf_op jit(solution)/shard_map/all_to_all | solution.py:150
  98.6 8.1 %select_bitcast_fusion.1 = (f32[1,16,32,128]{3,2,1,0:T(8,128)S(1)}, pred[16,32,128]{2,1,0:T(8,128)(4,1)S(1)}, pred[16,32,128]{2,1,0:T(8,128)(4,1)S(1)}, pred[16,...) fusion(f32[]{:T(128)} %bitcast.19, f32[]{:T(128)} %bitcast.18, ...), kind=kLoop, calls=%fused_computation.230 | loop fusion | flops 1572864 | bytes 1310768 | tf_op jit(solution)/shard_map/stack | solution.py:226
  106.7 7.7 %select_bitcast_fusion = f32[1,16,32,128]{3,2,1,0:T(8,128)S(1)} fusion(pred[16,32,128]{2,1,0:T(8,128)(4,1)S(1)} %get-tuple-element.16, pred[16,32,128]{2,1,0:T(8,128)(4,1)S(1)} %get-tuple-element.15, pred[16,32,128]{2,1,0:T(8,128)(4,1)S(1)} %get-tuple-element.14, pred[16,32,128]{2,1,0:T(8,128)(4,1)S(1)} %get-tuple-element.13, ...), kind=kLoop, calls=%fused_computation.229 | loop fusion | flops 786432 | bytes 1048624 | tf_op jit(solution)/shard_map/stack | solution.py:226
  115.4 2.9 collective-permute-start
  127.2 3.1 reduce
  130.4 5.1 %reshape.1300 = f32[2048,2,1,2,32]{4,3,2,1,0:T(2,128)} reshape(f32[16,16384]{1,0:T(8,128)S(1)} %reduce) | data formatting | bytes 2097152
  135.4 5.2 %copy.330 = f32[2,2,1,32,16,128]{5,3,4,1,2,0:T(8,128)S(1)} copy(f32[2,2,1,32,16,128]{3,1,0,5,4,2:T(2,128)} %bitcast.564) | data formatting | bytes 2097152 | tf_op jit(solution)/shard_map/all_to_all | solution.py:150
  149.1 6.5 %all-to-all-start.3 = ((f32[2,2,1,512,128]{4,1,2,0,3:T(2,128)}), f32[2,2,1,512,128]{4,1,2,0,3:T(2,128)S(1)}, u32[]{:S(2)}, u32[]{:S(2)}) async-start(f32[2,2,1,512,128]{4,1,2,0,3:T(2,128)} %copy.337), calls=%async_computation.3 | async-start | bytes 2097152 | tf_op jit(solution)/shard_map/all_to_all | solution.py:153
  155.6 2.3 fusion.28
  161.3 9.6 %collective-permute-done.2 = f32[2,16,16,128]{3,2,1,0:T(8,128)S(1)} collective-permute-done((f32[2,16,16,128]{3,2,1,0:T(8,128)S(1)}, f32[2,16,16,128]{3,2,1,0:T(8,128)S(1)}, u32[]{:S(2)}, u32[]{:S(2)}) %collective-permute-start.2) | collective-permute-done | bytes 262176 | tf_op jit(solution)/shard_map/ppermute | solution.py:21
  181.5 20.8 %all_to_all.96 = f32[2,2,16,32,128]{4,3,1,0,2:T(8,128)S(1)} all-to-all(f32[2,2,16,32,128]{4,3,1,0,2:T(8,128)S(1)} %copy.352), channel_id=1, replica_groups=mesh['row'=16,'col'=16] {'row'}, dimensions={2} | all-to-all | bytes 2097152 | tf_op jit(solution)/shard_map/all_to_all | solution.py:138
  211.3 7.5 %all-to-all-start.5 = ((f32[2,2,1,512,128]{4,1,2,0,3:T(2,128)}), f32[2,2,1,512,128]{4,1,2,0,3:T(2,128)S(1)}, u32[]{:S(2)}, u32[]{:S(2)}) async-start(f32[2,2,1,512,128]{4,1,2,0,3:T(2,128)} %pad_maximum_fusion.3), calls=%async_computation.5 | async-start | bytes 2097152 | tf_op jit(solution)/shard_map/all_to_all | solution.py:141
  218.8 25.9 %all-to-all-done.5 = f32[2,2,1,512,128]{4,1,2,0,3:T(2,128)S(1)} async-done(((f32[2,2,1,512,128]{4,1,2,0,3:T(2,128)}), f32[2,2,1,512,128]{4,1,2,0,3:T(2,128)S(1)}, u32[]{:S(2)}, u32[]{:S(2)}) %all-to-all-start.5) | async-done | bytes 1048608 | tf_op jit(solution)/shard_map/all_to_all | solution.py:141
  267.2 24.5 %all_to_all.97 = f32[16,1,8192]{2,1,0:T(1,128)S(1)} all-to-all(f32[16,1,8192]{2,1,0:T(1,128)S(1)} %reshape.1301), channel_id=1, replica_groups=mesh['row'=16,'col'=16] {'col'}, dimensions={0} | all-to-all | bytes 1048576 | tf_op jit(solution)/shard_map/all_to_all | solution.py:150
  301.7 6.1 %all-to-all-start.7 = ((f32[2,1,1,512,128]{4,2,1,0,3:T(1,128)}), f32[2,1,1,512,128]{4,2,1,0,3:T(1,128)S(1)}, u32[]{:S(2)}, u32[]{:S(2)}) async-start(f32[2,1,1,512,128]{4,2,1,0,3:T(1,128)} %copy.372), calls=%async_computation.7 | async-start | bytes 1048576 | tf_op jit(solution)/shard_map/all_to_all | solution.py:153
  307.9 9.7 %all-to-all-done.7 = f32[2,1,1,512,128]{4,2,1,0,3:T(1,128)S(1)} async-done(((f32[2,1,1,512,128]{4,2,1,0,3:T(1,128)}), f32[2,1,1,512,128]{4,2,1,0,3:T(1,128)S(1)}, u32[]{:S(2)}, u32[]{:S(2)}) %all-to-all-start.7) | async-done | bytes 524320 | tf_op jit(solution)/shard_map/all_to_all | solution.py:153
  (205 shorter events, 102.5 us)
Async XLA Ops:
  5.2 16.6 %all-to-all-start = ((f32[2,1,16,32,128]{4,3,1,0,2:T(8,128)}), f32[2,1,16,32,128]{4,3,1,0,2:T(8,128)S(1)}, u32[]{:S(2)}, u32[]{:S(2)}) async-start(f32[2,1,16,32,128]{4,3,1,0,2:T(8,128)} %copy.316), calls=%async_computation | async-start | bytes 1048576 | tf_op jit(solution)/shard_map/all_to_all | solution.py:138
  27.1 27.3 %all-to-all-start.1 = ((f32[2,1,1,512,128]{4,2,1,0,3:T(1,128)}), f32[2,1,1,512,128]{4,2,1,0,3:T(1,128)S(1)}, u32[]{:S(2)}, u32[]{:S(2)}) async-start(f32[2,1,1,512,128]{4,2,1,0,3:T(1,128)} %pad_maximum_fusion.6), calls=%async_computation.1 | async-start | bytes 1048576 | tf_op jit(solution)/shard_map/all_to_all | solution.py:141
  38.0 21.9 %copy-start.17 = (f32[32]{0:T(128)}, f32[32]{0:T(128)S(1)}, u32[]{:S(2)}) copy-start(f32[32]{0:T(128)S(1)} %get-tuple-element.82) | copy-start | bytes 388
  38.7 21.2 %copy-start.20 = (f32[32]{0:T(128)}, f32[32]{0:T(128)S(1)}, u32[]{:S(2)}) copy-start(f32[32]{0:T(128)S(1)} %get-tuple-element.85) | copy-start | bytes 388
  76.8 4.1 %copy-start = (f32[2,1,32,32,64]{2,0,4,3,1:T(2,128)S(1)}, f32[2,1,32,32,64]{2,0,4,3,1:T(2,128)}, u32[]{:S(2)}) copy-start(f32[2,1,32,32,64]{2,0,4,3,1:T(2,128)} %copy.390) | copy-start | bytes 1572868
  86.1 11.1 %copy-start.22 = (f32[12]{0:T(128)S(1)}, f32[12]{0:T(128)}, u32[]{:S(2)}) copy-start(f32[12]{0:T(128)} %param.14) | copy-start | bytes 148
  86.1 11.1 %copy-start.23 = (f32[12]{0:T(128)S(1)}, f32[12]{0:T(128)}, u32[]{:S(2)}) copy-start(f32[12]{0:T(128)} %param.15) | copy-start | bytes 148
  86.1 12.5 %copy-start.7 = (s32[16,32,128]{2,1,0:T(8,128)S(1)}, s32[16,32,128]{2,1,0:T(8,128)}, u32[]{:S(2)}) copy-start(s32[16,32,128]{2,1,0:T(8,128)} %param.9) | copy-start | bytes 786436
  92.7 27.9 %copy-start.11 = (s32[4]{0:T(128)S(1)}, s32[4]{0:T(128)}, u32[]{:S(2)}) copy-start(s32[4]{0:T(128)} %param.17) | copy-start | bytes 52
  92.7 33.7 %copy-start.16 = (f32[33]{0:T(128)S(1)}, f32[33]{0:T(128)}, u32[]{:S(2)}) copy-start(f32[33]{0:T(128)} %param.16) | copy-start | bytes 400
  92.7 34.0 %all-to-all-start.2 = ((f32[16,1,16384]{2,1,0:T(1,128)}), f32[16,1,16384]{2,1,0:T(1,128)S(1)}, u32[]{:S(2)}, u32[]{:S(2)}) async-start(f32[16,1,16384]{2,1,0:T(1,128)} %reshape.1299), calls=%async_computation.2 | async-start | bytes 2097152 | tf_op jit(solution)/shard_map/all_to_all | solution.py:150
  115.4 40.2 %collective-permute-start = (f32[2,16,32,16]{3,2,1,0:T(8,128)}, f32[2,16,32,16]{3,2,1,0:T(8,128)}, u32[]{:S(2)}, u32[]{:S(2)}) collective-permute-start(f32[2,16,32,16]{3,2,1,0:T(8,128)} %get-tuple-element.48), channel_id=1, source_target_pairs={{0,1},{1,2},{2,3},{3,4},{4,5},{5,6},{6,7},{7,8},{8,9},{9,10},{10,1... | collective-permute-start | bytes 196616 | tf_op jit(solution)/shard_map/ppermute | solution.py:21
  118.3 37.3 %collective-permute-start.1 = (f32[2,16,32,16]{3,2,1,0:T(8,128)S(1)}, f32[2,16,32,16]{3,2,1,0:T(8,128)}, u32[]{:S(2)}, u32[]{:S(2)}) collective-permute-start(f32[2,16,32,16]{3,2,1,0:T(8,128)S(1)} %get-tuple-element.49), channel_id=1, source_target_pairs={{1,0},{2,1},{3,2},{4,3},{5,4},{6,5},{7,6},{8,7},{9,8},{10,9},{11,1... | collective-permute-start | bytes 196616 | tf_op jit(solution)/shard_map/ppermute | solution.py:22
  149.1 24.1 %all-to-all-start.3 = ((f32[2,2,1,512,128]{4,1,2,0,3:T(2,128)}), f32[2,2,1,512,128]{4,1,2,0,3:T(2,128)S(1)}, u32[]{:S(2)}, u32[]{:S(2)}) async-start(f32[2,2,1,512,128]{4,1,2,0,3:T(2,128)} %copy.337), calls=%async_computation.3 | async-start | bytes 2097152 | tf_op jit(solution)/shard_map/all_to_all | solution.py:153
  158.0 12.9 %collective-permute-start.2 = (f32[2,16,16,128]{3,2,1,0:T(8,128)S(1)}, f32[2,16,16,128]{3,2,1,0:T(8,128)S(1)}, u32[]{:S(2)}, u32[]{:S(2)}) collective-permute-start(f32[2,16,16,128]{3,2,1,0:T(8,128)S(1)} %get-tuple-element.46), channel_id=1, source_target_pairs={{0,16},{16,32},{32,48},{48,64},{64,80},{80,96},{96,112},{112,128},... | collective-permute-start | bytes 786440 | tf_op jit(solution)/shard_map/ppermute | solution.py:21
  159.7 12.8 %collective-permute-start.3 = (f32[2,16,16,128]{3,2,1,0:T(8,128)S(1)}, f32[2,16,16,128]{3,2,1,0:T(8,128)S(1)}, u32[]{:S(2)}, u32[]{:S(2)}) collective-permute-start(f32[2,16,16,128]{3,2,1,0:T(8,128)S(1)} %get-tuple-element.47), channel_id=1, source_target_pairs={{16,0},{32,16},{48,32},{64,48},{80,64},{96,80},{112,96},{128,112},... | collective-permute-start | bytes 786440 | tf_op jit(solution)/shard_map/ppermute | solution.py:22
  173.1 4.6 %copy-start.2 = (f32[2,16,32,128]{3,2,1,0:T(8,128)}, f32[2,16,32,128]{3,2,1,0:T(8,128)S(1)}, u32[]{:S(2)}) copy-start(f32[2,16,32,128]{3,2,1,0:T(8,128)S(1)} %convolution_bitcast_fusion) | copy-start | bytes 1572868
  178.1 3.0 copy-start.4
  211.3 33.4 %all-to-all-start.5 = ((f32[2,2,1,512,128]{4,1,2,0,3:T(2,128)}), f32[2,2,1,512,128]{4,1,2,0,3:T(2,128)S(1)}, u32[]{:S(2)}, u32[]{:S(2)}) async-start(f32[2,2,1,512,128]{4,1,2,0,3:T(2,128)} %pad_maximum_fusion.3), calls=%async_computation.5 | async-start | bytes 2097152 | tf_op jit(solution)/shard_map/all_to_all | solution.py:141
  299.1 8.8 %copy-start.13 = (f32[32]{0:T(128)S(1)}, f32[32]{0:T(128)}, u32[]{:S(2)}) copy-start(f32[32]{0:T(128)} %multiply_exponential_fusion) | copy-start | bytes 388
  299.1 8.8 %copy-start.15 = (f32[128]{0:T(128)S(1)}, f32[128]{0:T(128)}, u32[]{:S(2)}) copy-start(f32[128]{0:T(128)} %multiply_exponential_fusion.1) | copy-start | bytes 1540
  300.4 18.7 %copy-start.1 = (f32[16,32,128]{2,1,0:T(8,128)S(1)}, f32[16,32,128]{2,1,0:T(8,128)}, u32[]{:S(2)}) copy-start(f32[16,32,128]{2,1,0:T(8,128)} %param.10) | copy-start | bytes 786436
  300.4 18.7 %copy-start.3 = (f32[2,16,32,128]{3,2,1,0:T(8,128)S(1)}, f32[2,16,32,128]{3,2,1,0:T(8,128)}, u32[]{:S(2)}) copy-start(f32[2,16,32,128]{3,2,1,0:T(8,128)} %copy-done.2) | copy-start | bytes 1572868
  301.7 15.9 %all-to-all-start.7 = ((f32[2,1,1,512,128]{4,2,1,0,3:T(1,128)}), f32[2,1,1,512,128]{4,2,1,0,3:T(1,128)S(1)}, u32[]{:S(2)}, u32[]{:S(2)}) async-start(f32[2,1,1,512,128]{4,2,1,0,3:T(1,128)} %copy.372), calls=%async_computation.7 | async-start | bytes 1048576 | tf_op jit(solution)/shard_map/all_to_all | solution.py:153
  (10 other events, 21.8 us)
where the time goes:
time: 326 us; the launch traced here: 320 us
  waiting for transfers between devices  71.5 us (22%)
  matrix products  66.5 us (20%)
  starting transfers between devices  49.2 us (15%)
  blocking collectives  45.2 us (14%)
  local copies, waits for them, and re-layouts  44 us (13%)
  other arithmetic  37.5 us (12%)
  between operations  6.28 us (2%)
    dot_general x78, matrix products, product(): return jnp.einsum(form, operand, matrix, precision=highest)  63.5 us
    all_to_all x2, waiting for transfers between devices, forward_rows(): lax.all_to_all(stacked, 'col', split_axis=3, concat_axis=4, tiled=True)  41.3 us
    all_to_all x1, blocking collectives, inverse_rows(): lax.all_to_all(stacked, 'col', split_axis=4, concat_axis=3, tiled=True)  24.5 us
    all_to_all x1, blocking collectives, forward_rows(): lax.all_to_all(stacked, 'row', split_axis=2, concat_axis=3, tiled=True)  20.8 us
    all_to_all x2, starting transfers between devices, forward_rows(): lax.all_to_all(stacked, 'col', split_axis=3, concat_axis=4, tiled=True)  18.1 us
    another operation x3, other arithmetic, on_device(): coefficients = jnp.stack([buoyancy, modulus])  16.8 us
    unnamed x55, local copies, waits for them, and re-layouts  15.8 us
    all_to_all x2, starting transfers between devices, inverse_rows(): lax.all_to_all(stacked, 'row', split_axis=3, concat_axis=2, tiled=True)  12.6 us
  transfers between devices with their start and end apart: 10, of which 6 were waited for; matrix products, arithmetic and copies ran while one was open for 15% of the time, Pallas kernels for 0%

commit v1 on v0

v1 whole, which is shorter than its diff:
```python
import functools
import math

import jax
import jax.numpy as jnp
import numpy as np
from jax import lax
from jax.experimental import pallas as pl
from jax.experimental.pallas import tpu as pltpu
from jax.sharding import PartitionSpec as P

time_step = 0.15
reference_speed = 2.0
absorption = 6.0
highest = lax.Precision.HIGHEST
MESH = pl.DeviceIdType.MESH

NZ, NY, NX = 16, 512, 2048
ROWS, COLS = 16, 16
YB, XB = NY // ROWS, NX // COLS
SLOTS = 8
f32, bf16 = jnp.float32, jnp.bfloat16


def split_table(table):
    high = table.astype(np.float32).astype(bf16)
    low = (table - high.astype(np.float64)).astype(np.float32).astype(bf16)
    return np.stack([high, low])


def row_tables():
    slot = np.arange(NY // 2)
    y = np.arange(NY)
    angle = 2.0 * np.pi * ((slot[:, None] * y[None, :]) % NY) / NY
    real, imag = np.cos(angle), -np.sin(angle)
    imag[0] = np.where(y % 2 == 0, 1.0, -1.0)
    order = lambda t: t.reshape(NY // 2 // SLOTS, SLOTS, NY)
    forward = np.stack([order(real), order(imag)], axis=1).reshape(NY, NY)
    weight = np.where(slot == 0, 1.0, 2.0) / NY
    inverse = np.stack([order(real * weight[:, None]), order(imag * weight[:, None])], axis=1)
    inverse = inverse.reshape(NY, NY).T
    wave = 2.0 * np.pi * slot / NY
    same = -wave * np.sin(0.5 * wave)
    cross = wave * np.cos(0.5 * wave)
    same_imag = same.copy()
    same_imag[0] = -np.pi
    wide = lambda v: np.broadcast_to(v.reshape(-1, SLOTS, 1), (NY // 2 // SLOTS, SLOTS, XB))
    derivative = np.stack([wide(same), wide(same_imag), wide(cross)]).astype(np.float32)
    return split_table(forward), split_table(inverse), derivative


def column_tables():
    x = np.arange(XB)
    angle = 2.0 * np.pi * ((x[:, None] * x[None, :]) % XB) / XB
    c, s = np.cos(angle), np.sin(angle)
    forward = np.block([[c, -s], [s, c]])
    inverse = np.block([[c, s], [-s, c]]) / NX
    kc = np.arange(COLS)
    twist = 2.0 * np.pi * (kc[:, None] * x[None, :]) / NX
    index = kc[:, None] + COLS * x[None, :]
    wave = 2.0 * np.pi * np.where(index < NX // 2, index, index - NX) / NX
    same = wave * np.sin(0.5 * wave)
    cross = wave * np.cos(0.5 * wave)
    small = np.stack([np.cos(twist), np.sin(twist), wave * wave, same, cross]).astype(np.float32)
    return split_table(forward), split_table(inverse), small


def scaled(value, factor):
    if abs(factor - 1.0) < 1e-12:
        return value
    if abs(factor + 1.0) < 1e-12:
        return -value
    return value * np.float32(factor)


def weighted(terms):
    total = None
    for value, factor in terms:
        if abs(factor) < 1e-12:
            continue
        if total is None:
            total = scaled(value, factor)
        elif abs(factor + 1.0) < 1e-12:
            total = total - value
        else:
            total = total + scaled(value, factor)
    return total


def cos16(n):
    return math.cos(2.0 * math.pi * (n % 16) / 16)


def sin16(n):
    return math.sin(2.0 * math.pi * (n % 16) / 16)


def depth_forward(p):
    even = [p[0]] + [p[n] + p[16 - n] for n in range(1, 8)] + [p[8]]
    odd = [None] + [p[n] - p[16 - n] for n in range(1, 8)]
    plus = [even[n] + even[8 - n] for n in range(4)] + [even[4]]
    minus = [even[n] - even[8 - n] for n in range(4)]
    odd_plus = [None] + [odd[n] + odd[8 - n] for n in range(1, 4)] + [odd[4]]
    odd_minus = [None] + [odd[n] - odd[8 - n] for n in range(1, 4)]

    def real_of(k):
        side = plus if k % 2 == 0 else minus
        return weighted([(side[n], cos16(k * n)) for n in range(len(side))])

    def imag_of(k):
        if k % 2 == 0:
            return weighted([(odd_minus[n], -sin16(k * n)) for n in range(1, 4)])
        return weighted([(odd_plus[n], -sin16(k * n)) for n in range(1, 5)])

    out = [real_of(0), real_of(8)]
    for k in range(1, 8):
        out += [real_of(k), imag_of(k)]
    return out


def depth_inverse(m):
    real = [m[0]] + [m[2 * k] for k in range(1, 8)] + [m[1]]
    imag = [None] + [m[2 * k + 1] for k in range(1, 8)]
    weight = [1.0 / 16] + [2.0 / 16] * 7 + [1.0 / 16]

    def terms(values, ids, n, wave):
        return weighted([(values[k], weight[k] * wave(k * n)) for k in ids])

    out = [None] * 16
    for n in range(0, 5):
        ce = terms(real, range(0, 9, 2), n, cos16)
        co = terms(real, range(1, 9, 2), n, cos16)
        so = terms(imag, range(1, 8, 2), n, lambda v: -sin16(v))
        se = terms(imag, range(2, 8, 2), n, lambda v: -sin16(v))
        near = ce if co is None else ce + co
        far = ce if co is None else ce - co
        if n == 0:
            out[0], out[8] = near, far
            continue
        if se is None:
            d_near, d_far = so, so
        else:
            d_near, d_far = so + se, so - se
        out[n], out[16 - n] = near + d_near, near - d_near
        if n < 4:
            out[8 - n], out[8 + n] = far + d_far, far - d_far
    return out


def depth_derivative(m, sign):
    out = [jnp.zeros_like(m[0]), m[1] * np.float32(-sign * math.pi)]
    for k in range(1, 8):
        wave = 2.0 * math.pi * k / 16
        a = np.float32(-sign * wave * math.sin(0.5 * wave))
        b = np.float32(wave * math.cos(0.5 * wave))
        out += [m[2 * k] * a - m[2 * k + 1] * b, m[2 * k + 1] * a + m[2 * k] * b]
    return out


def short_transform(values, sign):
    count = len(values)
    if count == 1:
        return values
    even = short_transform(values[0::2], sign)
    odd = short_transform(values[1::2], sign)
    out = [None] * count
    for k in range(count // 2):
        angle = sign * 2.0 * math.pi * k / count
        c, s = math.cos(angle), math.sin(angle)
        re, im = odd[k]
        if k == 0:
            tr, ti = re, im
        elif abs(c) < 1e-9:
            tr, ti = (-im, re) if s > 0 else (im, -re)
        elif abs(abs(c) - abs(s)) < 1e-9:
            h = np.float32(abs(c))
            cs, ss = (1 if c > 0 else -1), (1 if s > 0 else -1)
            first = re if cs > 0 else -re
            tr = (first - im if ss > 0 else first + im) * h
            second = im if cs > 0 else -im
            ti = (second + re if ss > 0 else second - re) * h
        else:
            tr = re * np.float32(c) - im * np.float32(s)
            ti = re * np.float32(s) + im * np.float32(c)
        er, ei = even[k]
        out[k] = (er + tr, ei + ti)
        out[k + count // 2] = (er - tr, ei - ti)
    return out


def halves(value):
    high = value.astype(bf16)
    low = (value - high.astype(f32)).astype(bf16)
    return high, low


def mm(a, b):
    return jnp.dot(a, b, preferred_element_type=f32)


def step_kernel(
    p_ref, vx_ref, vy_ref, vz_ref, b_ref, m_ref, dx_ref, dy_ref,
    fy_ref, gy_ref, yd_ref, wx_ref, ux_ref, xt_ref,
    po_ref, vxo_ref, vyo_ref, vzo_ref,
    row_out, row_in, col_out, col_in, bcol_out, bcol_in, brow_out, brow_in,
    kappa, xb, xs,
    send_sem, recv_sem,
):
    r, c = lax.axis_index("row"), lax.axis_index("col")
    j, h = r // 2, r % 2
    q = h * COLS + c

    barrier = pltpu.get_barrier_semaphore()

    def greet_row(i, carry):
        pl.semaphore_signal(barrier, inc=1, device_id=((r + i) % ROWS, c), device_id_type=MESH)
        return carry

    def greet_plane(i, carry):
        t = (q + i) % (2 * COLS)
        pl.semaphore_signal(
            barrier, inc=1, device_id=(2 * j + t // COLS, t % COLS), device_id_type=MESH
        )
        return carry

    lax.fori_loop(1, ROWS, greet_row, 0)
    lax.fori_loop(1, 2 * COLS, greet_plane, 0)

    def row_copy(src, dst, sem, i):
        t = (r + i) % ROWS
        return pltpu.make_async_remote_copy(
            src_ref=src.at[t], dst_ref=dst.at[r], send_sem=send_sem.at[sem],
            recv_sem=recv_sem.at[sem], device_id=(t, c), device_id_type=MESH,
        )

    def plane_copy(src, dst, sem, i):
        t = (q + i) % (2 * COLS)
        return pltpu.make_async_remote_copy(
            src_ref=src.at[t], dst_ref=dst.at[q], send_sem=send_sem.at[sem],
            recv_sem=recv_sem.at[sem], device_id=(2 * j + t // COLS, t % COLS),
            device_id_type=MESH,
        )

    def start_all(copy_of, src, dst, sem, count, own):
        def body(i, carry):
            copy_of(src, dst, sem, i).start()
            return carry

        lax.fori_loop(1, count, body, 0)
        dst[own] = src[own]

    def whole(src, dst, sem, count):
        span = pl.ds(0, count - 1)
        return pltpu.make_async_remote_copy(
            src_ref=src.at[span], dst_ref=dst.at[span], send_sem=send_sem.at[sem],
            recv_sem=recv_sem.at[sem], device_id=((r + 1) % ROWS, c), device_id_type=MESH,
        )

    def send_row(f):
        start_all(row_copy, row_out.at[f], row_in.at[f], f, ROWS, r)

    def send_col(f):
        start_all(plane_copy, col_out.at[f], col_in.at[f], 4 + f, 2 * COLS, q)

    def send_bcol(f):
        start_all(plane_copy, bcol_out.at[f], bcol_in.at[f], 7 + f, 2 * COLS, q)

    def send_brow(f):
        start_all(row_copy, brow_out.at[f], brow_in.at[f], 10 + f, ROWS, r)

    def all_of(kind, f):
        src, dst, base, count = {
            "row": (row_out, row_in, 0, ROWS),
            "col": (col_out, col_in, 4, 2 * COLS),
            "bcol": (bcol_out, bcol_in, 7, 2 * COLS),
            "brow": (brow_out, brow_in, 10, ROWS),
        }[kind]
        return whole(src.at[f], dst.at[f], base + f, count)

    def arrived(kind, f):
        all_of(kind, f).wait_recv()

    def load(ref, rows):
        return [ref[z, rows, :] for z in range(NZ)]

    def store(ref, rows, planes):
        for z in range(NZ):
            ref[z, rows, :] = planes[z]

    def chunks(body):
        def step(i, carry):
            body(pl.ds(pl.multiple_of(i * 8, 8), 8))
            return carry

        lax.fori_loop(0, YB // 8, step, 0)

    def pressure_planes(rows):
        store(row_out.at[0], rows, depth_forward(load(p_ref, rows)))

    chunks(pressure_planes)

    lane_rows = lax.broadcasted_iota(jnp.int32, (SLOTS, XB), 0)
    slot = q * SLOTS + lane_rows
    one, zero = jnp.ones((SLOTS, XB), f32), jnp.zeros((SLOTS, XB), f32)
    first = jnp.where(slot == 0, one, zero)
    flat = jnp.where(jnp.full((SLOTS, XB), j, jnp.int32) == 0, one, zero)
    general = (1.0 - first) * (1.0 - flat)
    half_general = 0.5 * general
    first_deep = first * (1.0 - flat)
    first_flat = first * flat
    rest_flat = flat * (1.0 - first)
    own_imag = first_deep + rest_flat
    not_first = 1.0 - first
    not_flat = 1.0 - flat

    pi2 = np.float32(math.pi * math.pi)
    ky = slot.astype(f32) * np.float32(2.0 * math.pi / NY)
    kz = jnp.full((SLOTS, XB), j, jnp.int32).astype(f32) * np.float32(2.0 * math.pi / NZ)
    low = ky * ky + kz * kz
    top = low + pi2 * (first_deep + flat)
    extra = pi2 + jnp.where(lane_rows == 0, zero, pi2 * one)
    scale = np.float32((0.5 * reference_speed * time_step) ** 2)

    def fill_kappa(kc, carry):
        kx2 = xt_ref[2, pl.ds(kc, 1), :]
        for g, part in enumerate((low, top, extra)):
            v2 = scale * (kx2 + part)
            series = 1.0 + v2 * np.float32(-1.0 / 110.0)
            series = 1.0 + v2 * np.float32(-1.0 / 72.0) * series
            series = 1.0 + v2 * np.float32(-1.0 / 42.0) * series
            series = 1.0 + v2 * np.float32(-1.0 / 20.0) * series
            kappa[g, kc] = 1.0 + v2 * np.float32(-1.0 / 6.0) * series
        return carry

    lax.fori_loop(0, COLS, fill_kappa, 0)

    pl.semaphore_wait(barrier, ROWS - 1 + 2 * COLS - 1)
    send_row(0)

    def lines(ref, f):
        return ref[f].reshape(NY, XB)

    def row_product(table, values):
        parts = [halves(v) for v in values]
        high = [part[0] for part in parts]
        low_part = [part[1] for part in parts]
        if len(values) == 1:
            both = mm(table[0], jnp.concatenate([high[0], low_part[0]], axis=1))
            return [both[:, :XB] + both[:, XB:] + mm(table[1], high[0])]
        high = jnp.concatenate(high, axis=1)
        low_part = jnp.concatenate(low_part, axis=1)
        result = mm(table[0], high) + mm(table[0], low_part) + mm(table[1], high)
        return [result[:, :XB], result[:, XB:]]

    def y_derivative(value, sign):
        parts = value.reshape(NY // 2 // SLOTS, 2, SLOTS, XB)
        re, im = parts[:, 0], parts[:, 1]
        same, same_imag, cross = yd_ref[0], yd_ref[1], yd_ref[2]
        if sign > 0:
            out = [re * same - im * cross, im * same_imag + re * cross]
        else:
            out = [-(re * same + im * cross), re * cross - im * same_imag]
        return jnp.stack(out, axis=1).reshape(NY, XB)

    def x_forward(f):
        for n in range(COLS):
            rr, ri = col_in[f, n, 0:8, :], col_in[f, n, 8:16, :]
            ir, ii = col_in[f, COLS + n, 0:8, :], col_in[f, COLS + n, 8:16, :]
            xb[0, 0, n] = rr - general * ii
            xb[0, 1, n] = not_first * ri + not_flat * ir
            xb[1, 0, n] = general * (rr + ii) + first_deep * ri + flat * ir
            xb[1, 1, n] = general * (ir - ri) + own_imag * ii
            xb[2, 0, n] = first_flat * ri + pltpu.roll(first_flat * ii, 1, 0)
            xb[2, 1, n] = zero

        def group(g, carry):
            values = [(xb[g, 0, n], xb[g, 1, n]) for n in range(COLS)]
            values = short_transform(values, -1.0)
            for kc in range(COLS):
                re, im = values[kc]
                cs, sn = xt_ref[0, kc : kc + 1, :], xt_ref[1, kc : kc + 1, :]
                xs[0, g, kc, :, :XB] = re * cs + im * sn
                xs[0, g, kc, :, XB:] = im * cs - re * sn
            return carry

        lax.fori_loop(0, 3, group, 0)
        high, low_part = halves(xs[0].reshape(3 * COLS * SLOTS, 2 * XB))
        out = mm(high, wx_ref[0]) + mm(low_part, wx_ref[0]) + mm(high, wx_ref[1])
        return out.reshape(3, COLS, SLOTS, 2 * XB)

    def x_derivative(re, im, sign):
        same = xt_ref[3][None, :, None, :]
        cross = xt_ref[4][None, :, None, :]
        if sign > 0:
            return -(re * same + im * cross), re * cross - im * same
        return re * same - im * cross, im * same + re * cross

    def x_inverse(value, f):
        high, low_part = halves(value.reshape(3 * COLS * SLOTS, 2 * XB))
        out = mm(high, ux_ref[0]) + mm(low_part, ux_ref[0]) + mm(high, ux_ref[1])
        xs[0] = out.reshape(3, COLS, SLOTS, 2 * XB)

        def group(g, carry):
            values = []
            for kc in range(COLS):
                re, im = xs[0, g, kc, :, :XB], xs[0, g, kc, :, XB:]
                cs, sn = xt_ref[0, kc : kc + 1, :], xt_ref[1, kc : kc + 1, :]
                values.append((re * cs - im * sn, im * cs + re * sn))
            values = short_transform(values, 1.0)
            for n in range(COLS):
                xb[g, 0, n] = values[n][0]
                xb[g, 1, n] = values[n][1]
            return carry

        lax.fori_loop(0, 3, group, 0)
        for n in range(COLS):
            lr, li = xb[0, 0, n], xb[0, 1, n]
            hr, hi = xb[1, 0, n], xb[1, 1, n]
            xr = xb[2, 0, n]
            bcol_out[f, n, 0:8, :] = lr + half_general * (hr - lr)
            bcol_out[f, n, 8:16, :] = (
                half_general * (li - hi) + first_deep * hr + rest_flat * li + first_flat * xr
            )
            bcol_out[f, COLS + n, 0:8, :] = half_general * (li + hi) + first_deep * li + flat * hr
            bcol_out[f, COLS + n, 8:16, :] = (
                half_general * (hr - lr) + own_imag * hi + first_flat * pltpu.roll(xr, 7, 0)
            )

    arrived("row", 0)
    col_out[0] = row_product(fy_ref, [lines(row_in, 0)])[0].reshape(2 * COLS, 2 * SLOTS, XB)
    send_col(0)

    arrived("col", 0)
    spectrum = x_forward(0)
    re, im = spectrum[..., :XB] * kappa[...], spectrum[..., XB:] * kappa[...]
    dre, dim = x_derivative(re, im, 1)
    x_inverse(jnp.concatenate([dre, dim], axis=-1), 0)
    send_bcol(0)
    x_inverse(jnp.concatenate([re, im], axis=-1), 1)
    send_bcol(1)

    arrived("bcol", 0)
    brow_out[0] = row_product(gy_ref, [lines(bcol_in, 0)])[0].reshape(ROWS, YB, XB)
    send_brow(0)

    dx = dx_ref[0:8, :]

    arrived("brow", 0)

    def update_x(rows):
        grad = depth_inverse(load(brow_in.at[0], rows))
        fresh = []
        for z in range(NZ):
            change = time_step * b_ref[z, rows, :] * grad[z]
            fresh.append(dx * (dx * vx_ref[z, rows, :] - change))
        store(vxo_ref, rows, fresh)
        store(row_out.at[1], rows, depth_forward(fresh))

    chunks(update_x)
    send_row(1)

    arrived("bcol", 1)
    flow = lines(bcol_in, 1)
    plain, slope = row_product(gy_ref, [flow, y_derivative(flow, 1)])
    brow_out[1] = slope.reshape(ROWS, YB, XB)
    send_brow(1)
    brow_out[2] = plain.reshape(ROWS, YB, XB)
    send_brow(2)

    arrived("row", 1)
    col_out[1] = row_product(fy_ref, [lines(row_in, 1)])[0].reshape(2 * COLS, 2 * SLOTS, XB)
    send_col(1)

    arrived("brow", 1)

    def update_y(rows):
        grad = depth_inverse(load(brow_in.at[1], rows))
        dy = dy_ref[rows, :]
        fresh = []
        for z in range(NZ):
            change = time_step * b_ref[z, rows, :] * grad[z]
            fresh.append(dy * (dy * vy_ref[z, rows, :] - change))
        store(vyo_ref, rows, fresh)
        store(row_out.at[2], rows, depth_forward(fresh))

    chunks(update_y)
    send_row(2)

    arrived("brow", 2)

    def update_z(rows):
        grad = depth_inverse(depth_derivative(load(brow_in.at[2], rows), 1))
        fresh = []
        for z in range(NZ):
            fresh.append(vz_ref[z, rows, :] - time_step * b_ref[z, rows, :] * grad[z])
        store(vzo_ref, rows, fresh)
        store(row_out.at[3], rows, depth_derivative(depth_forward(fresh), -1))

    chunks(update_z)
    send_row(3)

    arrived("row", 2)
    arrived("row", 3)
    across, deep = row_product(fy_ref, [lines(row_in, 2), lines(row_in, 3)])
    summed = deep + y_derivative(across, -1)
    col_out[2] = summed.reshape(2 * COLS, 2 * SLOTS, XB)
    send_col(2)

    arrived("col", 1)
    flow_x = x_forward(1)
    tre, tim = x_derivative(flow_x[..., :XB], flow_x[..., XB:], -1)
    arrived("col", 2)
    rest = x_forward(2)
    tre = (tre + rest[..., :XB]) * kappa[...]
    tim = (tim + rest[..., XB:]) * kappa[...]
    x_inverse(jnp.concatenate([tre, tim], axis=-1), 2)
    send_bcol(2)

    arrived("bcol", 2)
    brow_out[3] = row_product(gy_ref, [lines(bcol_in, 2)])[0].reshape(ROWS, YB, XB)
    send_brow(3)

    arrived("brow", 3)

    def update_p(rows):
        divergence = depth_inverse(load(brow_in.at[3], rows))
        both = dx * dy_ref[rows, :]
        for z in range(NZ):
            change = time_step * m_ref[z, rows, :] * divergence[z]
            po_ref[z, rows, :] = both * (both * p_ref[z, rows, :] - change)

    chunks(update_p)

    for kind, number in (("row", 4), ("col", 3), ("bcol", 3), ("brow", 4)):
        for f in range(number):
            all_of(kind, f).wait_send()


def extended(array, sides, width):
    for axis, dim in sides:
        size, length = (lax.axis_size(axis), array.shape[dim])
        up = [(i, (i + 1) % size) for i in range(size)]
        down = [(j, i) for i, j in up]
        last = lax.slice_in_dim(array, length - width, length, axis=dim)
        initial = lax.slice_in_dim(array, 0, width, axis=dim)
        before = lax.ppermute(last, axis, up)
        after = lax.ppermute(initial, axis, down)
        array = jnp.concatenate([before, array, after], axis=dim)
    return array


def band_matrix(filter_taps, extent):
    tap_count = filter_taps.shape[0]
    offset = (
        jnp.arange(extent + tap_count - 1, dtype=jnp.int32)[:, None]
        - jnp.arange(extent, dtype=jnp.int32)[None, :]
    )
    selected = offset[:, :, None] == jnp.arange(tap_count, dtype=jnp.int32)[None, None, :]
    return jnp.sum(jnp.where(selected, filter_taps[None, None, :], 0.0), axis=2)


def absorber(position, length, low_width, high_width):
    low_part = jnp.maximum(low_width - position, 0).astype(f32) / low_width.astype(f32)
    high_part = jnp.maximum(position - (length - 1 - high_width), 0).astype(
        f32
    ) / high_width.astype(f32)
    damping = absorption * reference_speed * (low_part**4 + high_part**4)
    return jnp.exp(-0.5 * time_step * damping)


def on_device(
    labels, pressure, velocity_x, velocity_y, velocity_z,
    speed_table, density_table, filter_taps, layer_width,
):
    planes, height, breadth = pressure.shape
    buoyancy_of = 1.0 / density_table
    modulus_of = density_table * speed_table * speed_table
    buoyancy = jnp.zeros(pressure.shape, f32)
    modulus = jnp.zeros(pressure.shape, f32)
    for label_id in range(speed_table.shape[0]):
        matches = labels == label_id
        buoyancy = jnp.where(matches, buoyancy_of[label_id], buoyancy)
        modulus = jnp.where(matches, modulus_of[label_id], modulus)
    coefficients = jnp.stack([buoyancy, modulus])
    reach = filter_taps.shape[0] // 2
    across = band_matrix(filter_taps, breadth)
    downward = band_matrix(filter_taps, height)
    padded = extended(coefficients, (("col", 3),), reach)
    smoothed = jnp.einsum("fzyj,ji->fzyi", padded, across, precision=highest)
    padded = extended(smoothed, (("row", 2),), reach)
    smoothed = jnp.einsum("fzjx,jy->fzyx", padded, downward, precision=highest)
    buoyancy = smoothed[0]
    modulus = smoothed[1]
    column_ids = lax.axis_index("col") * breadth + jnp.arange(breadth, dtype=jnp.int32)
    row_ids = lax.axis_index("row") * height + jnp.arange(height, dtype=jnp.int32)
    damp_x = absorber(column_ids, NX, layer_width[0], layer_width[1])
    damp_y = absorber(row_ids, NY, layer_width[2], layer_width[3])
    damp_x = jnp.broadcast_to(damp_x[None, :], (8, breadth))
    damp_y = jnp.broadcast_to(damp_y[:, None], (height, breadth))

    fy, gy, yd = row_tables()
    wx, ux, xt = column_tables()
    brick = jax.ShapeDtypeStruct(pressure.shape, f32)
    row_buffer = lambda n: pltpu.VMEM((n, ROWS, YB, XB), f32)
    col_buffer = lambda n: pltpu.VMEM((n, 2 * COLS, 2 * SLOTS, XB), f32)
    return pl.pallas_call(
        step_kernel,
        out_shape=(brick,) * 4,
        in_specs=[pl.BlockSpec(memory_space=pltpu.VMEM)] * 14,
        out_specs=(pl.BlockSpec(memory_space=pltpu.VMEM),) * 4,
        scratch_shapes=[
            row_buffer(4), row_buffer(4), col_buffer(3), col_buffer(3),
            col_buffer(3), col_buffer(3), row_buffer(4), row_buffer(4),
            pltpu.VMEM((3, COLS, SLOTS, XB), f32),
            pltpu.VMEM((3, 2, COLS, SLOTS, XB), f32),
            pltpu.VMEM((1, 3, COLS, SLOTS, 2 * XB), f32),
            pltpu.SemaphoreType.DMA((14,)),
            pltpu.SemaphoreType.DMA((14,)),
        ],
        compiler_params=pltpu.CompilerParams(
            collective_id=0, has_side_effects=True, vmem_limit_bytes=48 * 1024 * 1024
        ),
    )(
        pressure, velocity_x, velocity_y, velocity_z, buoyancy, modulus, damp_x, damp_y,
        jnp.asarray(fy), jnp.asarray(gy), jnp.asarray(yd),
        jnp.asarray(wx), jnp.asarray(ux), jnp.asarray(xt),
    )


def solution(mesh):
    brick = P(None, "row", "col")
    return jax.shard_map(
        on_device,
        mesh=mesh,
        in_specs=(brick,) * 5 + (P(),) * 4,
        out_specs=(brick,) * 4,
        check_vma=False,
    )
```

time: 326 us -> 154 us (0.47); the launches traced: 320 us -> 154 us
  Pallas kernels: 0 us -> 91.1 us
  matrix products: 66.5 us -> 1.76 us
  waiting for transfers between devices: 71.5 us -> 19.6 us
  blocking collectives: 45.2 us -> 0 us
  local copies, waits for them, and re-layouts: 44 us -> 5.03 us
  starting transfers between devices: 49.2 us -> 12.1 us
  other arithmetic: 37.5 us -> 19.7 us
    pallas_call x0 -> x1, Pallas kernels: none -> 91.1 us  [on_device(): pl.pallas_call(step_kernel, out_shape=(brick,) * 4, in_specs=[pl.BlockSpe...]
    dot_general x78 -> x0, matrix products: 63.5 us -> none  [product(): return jnp.einsum(form, operand, matrix, precision=highest)]
    all_to_all x6 -> x0, waiting for transfers between devices: 60.4 us -> none  [the longest x2 41.3 us: forward_rows(): lax.all_to_all(stacked, 'col', split_axis=3, concat_axis=4, tiled=True)]
    all_to_all x2 -> x0, blocking collectives: 45.2 us -> none  [the longest x1 24.5 us: inverse_rows(): lax.all_to_all(stacked, 'col', split_axis=4, concat_axis=3, tiled=True)]
    all_to_all x6 -> x0, starting transfers between devices: 42.2 us -> none  [the longest x2 18.1 us: forward_rows(): lax.all_to_all(stacked, 'col', split_axis=3, concat_axis=4, tiled=True)]
    another operation x15 -> x0, local copies, waits for them, and re-layouts: 16.4 us -> none  [the longest x5 9.41 us: inverse_rows(): stacked = jnp.stack([pieces[0], pieces[1]])]
    unnamed x55 -> x28, local copies, waits for them, and re-layouts: 15.8 us -> 2.88 us
    all_to_all x5 -> x0, local copies, waits for them, and re-layouts: 7.44 us -> none  [the longest x3 6.52 us: inverse_rows(): lax.all_to_all(stacked, 'col', split_axis=4, concat_axis=3, tiled=True)]
  transfers between devices with their start and end apart: 10 -> 4, of which waited for: 6 -> 4; matrix products, arithmetic and copies ran while one was open for 15% -> 2% of each run, Pallas kernels for 0% -> 0%
where the time goes in v1:
time: 154 us
  Pallas kernels  91.1 us (59%)
  other arithmetic  19.7 us (13%)
  waiting for transfers between devices  19.6 us (13%)
  starting transfers between devices  12.1 us (8%)
  local copies, waits for them, and re-layouts  5.03 us (3%)
  between operations  4.79 us (3%)
  matrix products  1.76 us (1%)
    pallas_call x1, Pallas kernels, on_device(): pl.pallas_call(step_kernel, out_shape=(brick,) * 4, in_specs=[pl.BlockSpe...  91.1 us
    another operation x3, other arithmetic, on_device(): coefficients = jnp.stack([buoyancy, modulus])  17.2 us
    ppermute x2, waiting for transfers between devices, extended(): before = lax.ppermute(last, axis, up)  13.4 us
    ppermute x2, starting transfers between devices, extended(): before = lax.ppermute(last, axis, up)  6.71 us
    ppermute x2, waiting for transfers between devices, extended(): after = lax.ppermute(initial, axis, down)  6.2 us
    ppermute x2, starting transfers between devices, extended(): after = lax.ppermute(initial, axis, down)  5.38 us
  transfers between devices with their start and end apart: 4, of which 4 were waited for; matrix products, arithmetic and copies ran while one was open for 2% of the time, Pallas kernels for 0%

profile of v1, /device:TPU:1, one launch (start us, length us, event | category | flops | bytes accessed | tf_op | source)
XLA Modules:
  0.0 154.0 jit_solution(980898120404550402)
XLA Ops:
  0.6 0.7 multiply_multiply_fusion
  1.3 0.7 fusion.26
  2.0 0.7 fusion.25
  2.7 9.1 %select_bitcast_fusion.1 = (f32[1,16,32,128]{3,2,1,0:T(8,128)S(1)}, pred[16,32,128]{2,1,0:T(8,128)(4,1)S(1)}, pred[16,32,128]{2,1,0:T(8,128)(4,1)S(1)}, pred[16,...) fusion(f32[]{:T(128)} %bitcast.13, f32[]{:T(128)} %bitcast.12, ...), kind=kLoop, calls=%fused_computation.23 | loop fusion | flops 1572864 | bytes 1310768 | tf_op jit(solution)/shard_map/stack | solution.py:584
  11.8 7.9 %select_bitcast_fusion = f32[1,16,32,128]{3,2,1,0:T(8,128)S(1)} fusion(pred[16,32,128]{2,1,0:T(8,128)(4,1)S(1)} %get-tuple-element.16, pred[16,32,128]{2,1,0:T(8,128)(4,1)S(1)} %get-tuple-element.15, pred[16,32,128]{2,1,0:T(8,128)(4,1)S(1)} %get-tuple-element.14, pred[16,32,128]{2,1,0:T(8,128)(4,1)S(1)} %get-tuple-element.13, ...), kind=kLoop, calls=%fused_computation.22 | loop fusion | flops 786432 | bytes 1048624 | tf_op jit(solution)/shard_map/stack | solution.py:584
  19.7 0.2 slice_maximum_fusion
  19.9 3.6 %collective-permute-start = (f32[2,16,32,16]{3,2,1,0:T(8,128)S(1)}, f32[2,16,32,16]{3,2,1,0:T(8,128)S(1)}, u32[]{:S(2)}, u32[]{:S(2)}) collective-permute-start(f32[2,16,32,16]{3,2,1,0:T(8,128)S(1)} %get-tuple-element.21), channel_id=1, source_target_pairs={{0,1},{1,2},{2,3},{3,4},{4,5},{5,6},{6,7},{7,8},{8,9},{9,10},{10,1... | collective-permute-start | bytes 196616 | tf_op jit(solution)/shard_map/ppermute | solution.py:546
  23.6 5.4 %collective-permute-start.1 = (f32[2,16,32,16]{3,2,1,0:T(8,128)S(1)}, f32[2,16,32,16]{3,2,1,0:T(8,128)S(1)}, u32[]{:S(2)}, u32[]{:S(2)}) collective-permute-start(f32[2,16,32,16]{3,2,1,0:T(8,128)S(1)} %get-tuple-element.22), channel_id=1, source_target_pairs={{1,0},{2,1},{3,2},{4,3},{5,4},{6,5},{7,6},{8,7},{9,8},{10,9},{11,1... | collective-permute-start | bytes 196616 | tf_op jit(solution)/shard_map/ppermute | solution.py:547
  29.0 0.6 fusion.24
  33.5 0.3 select_reduce_fusion
  33.8 0.7 multiply_exponential_fusion
  34.5 10.9 %collective-permute-done = f32[2,16,32,16]{3,2,1,0:T(8,128)S(1)} collective-permute-done((f32[2,16,32,16]{3,2,1,0:T(8,128)S(1)}, f32[2,16,32,16]{3,2,1,0:T(8,128)S(1)}, u32[]{:S(2)}, u32[]{:S(2)}) %collective-permute-start) | collective-permute-done | bytes 65568 | tf_op jit(solution)/shard_map/ppermute | solution.py:546
  45.4 3.4 %collective-permute-done.1 = f32[2,16,32,16]{3,2,1,0:T(8,128)S(1)} collective-permute-done((f32[2,16,32,16]{3,2,1,0:T(8,128)S(1)}, f32[2,16,32,16]{3,2,1,0:T(8,128)S(1)}, u32[]{:S(2)}, u32[]{:S(2)}) %collective-permute-start.1) | collective-permute-done | bytes 65568 | tf_op jit(solution)/shard_map/ppermute | solution.py:547
  48.9 1.1 fusion
  50.1 3.1 %collective-permute-start.2 = (f32[2,16,16,128]{3,2,1,0:T(8,128)S(1)}, f32[2,16,16,128]{3,2,1,0:T(8,128)S(1)}, u32[]{:S(2)}, u32[]{:S(2)}) collective-permute-start(f32[2,16,16,128]{3,2,1,0:T(8,128)S(1)} %get-tuple-element.19), channel_id=1, source_target_pairs={{0,16},{16,32},{32,48},{48,64},{64,80},{80,96},{96,112},{112,128},... | collective-permute-start | bytes 786440 | tf_op jit(solution)/shard_map/ppermute | solution.py:546
  53.2 0.7 multiply_exponential_fusion.1
  54.0 2.4 %collective-permute-done.2 = f32[2,16,16,128]{3,2,1,0:T(8,128)S(1)} collective-permute-done((f32[2,16,16,128]{3,2,1,0:T(8,128)S(1)}, f32[2,16,16,128]{3,2,1,0:T(8,128)S(1)}, u32[]{:S(2)}, u32[]{:S(2)}) %collective-permute-start.2) | collective-permute-done | bytes 262176 | tf_op jit(solution)/shard_map/ppermute | solution.py:546
  56.5 2.8 %collective-permute-done.3 = f32[2,16,16,128]{3,2,1,0:T(8,128)S(1)} collective-permute-done((f32[2,16,16,128]{3,2,1,0:T(8,128)S(1)}, f32[2,16,16,128]{3,2,1,0:T(8,128)S(1)}, u32[]{:S(2)}, u32[]{:S(2)}) %collective-permute-start.3) | collective-permute-done | bytes 262176 | tf_op jit(solution)/shard_map/ppermute | solution.py:547
  59.3 0.6 convolution_bitcast_fusion
  60.1 91.1 %shard_map.174 = (f32[16,32,128]{2,1,0:T(8,128)S(1)}, f32[16,32,128]{2,1,0:T(8,128)S(1)}, f32[16,32,128]{2,1,0:T(8,128)S(1)}, f32[16,32,128]{2,1,0:T(8,128)S(1)}) custom-call(f32[16,32,128]{2,1,0:T(8,128)S(1)} %copy-done.3, f32[16,32,128]{2,1,0:T(8,128)S(1)} %copy-done.4, f32[16,32,128]{2,1,0:T(8,128)S(1)} %copy-done.5, f32[16,32,128]{2,1,0:T(8,128)S(1)} %copy-done.6, ...), custom_call_target="tpu_custom_call" | custom-call | tf_op jit(solution)/shard_map/pallas_call | solution.py:606
  151.2 0.7 copy.25
  151.9 0.7 copy.26
  152.6 0.7 copy.27
  153.3 0.7 copy.28
  (32 shorter events, 0.4 us)
Async XLA Ops:
  19.7 9.3 %copy-start.10 = (s32[4]{0:T(128)S(1)}, s32[4]{0:T(128)}, u32[]{:S(2)}) copy-start(s32[4]{0:T(128)} %param.23) | copy-start | bytes 52
  19.7 13.8 %copy-start.11 = (f32[33]{0:T(128)S(1)}, f32[33]{0:T(128)}, u32[]{:S(2)}) copy-start(f32[33]{0:T(128)} %param.22) | copy-start | bytes 400
  19.9 25.5 %collective-permute-start = (f32[2,16,32,16]{3,2,1,0:T(8,128)S(1)}, f32[2,16,32,16]{3,2,1,0:T(8,128)S(1)}, u32[]{:S(2)}, u32[]{:S(2)}) collective-permute-start(f32[2,16,32,16]{3,2,1,0:T(8,128)S(1)} %get-tuple-element.21), channel_id=1, source_target_pairs={{0,1},{1,2},{2,3},{3,4},{4,5},{5,6},{6,7},{7,8},{8,9},{9,10},{10,1... | collective-permute-start | bytes 196616 | tf_op jit(solution)/shard_map/ppermute | solution.py:546
  23.6 25.3 %collective-permute-start.1 = (f32[2,16,32,16]{3,2,1,0:T(8,128)S(1)}, f32[2,16,32,16]{3,2,1,0:T(8,128)S(1)}, u32[]{:S(2)}, u32[]{:S(2)}) collective-permute-start(f32[2,16,32,16]{3,2,1,0:T(8,128)S(1)} %get-tuple-element.22), channel_id=1, source_target_pairs={{1,0},{2,1},{3,2},{4,3},{5,4},{6,5},{7,6},{8,7},{9,8},{10,9},{11,1... | collective-permute-start | bytes 196616 | tf_op jit(solution)/shard_map/ppermute | solution.py:547
  48.8 11.2 %copy-start.7 = (bf16[2,256,256]{2,1,0:T(8,128)(2,1)S(1)}, bf16[2,256,256]{2,1,0:T(8,128)(2,1)}, u32[]{:S(2)}) copy-start(bf16[2,256,256]{2,1,0:T(8,128)(2,1)} %constant.70.clone.wx_ref) | copy-start | bytes 786436
  48.9 11.2 %copy-start.8 = (bf16[2,256,256]{2,1,0:T(8,128)(2,1)S(1)}, bf16[2,256,256]{2,1,0:T(8,128)(2,1)}, u32[]{:S(2)}) copy-start(bf16[2,256,256]{2,1,0:T(8,128)(2,1)} %constant.71.clone.ux_ref) | copy-start | bytes 786436
  50.0 10.0 %copy-start.3 = (f32[16,32,128]{2,1,0:T(8,128)S(1)}, f32[16,32,128]{2,1,0:T(8,128)}, u32[]{:S(2)}) copy-start(f32[16,32,128]{2,1,0:T(8,128)} %p_ref.1) | copy-start | bytes 786436
  50.0 10.0 %copy-start.4 = (f32[16,32,128]{2,1,0:T(8,128)S(1)}, f32[16,32,128]{2,1,0:T(8,128)}, u32[]{:S(2)}) copy-start(f32[16,32,128]{2,1,0:T(8,128)} %vx_ref.1) | copy-start | bytes 786436
  50.0 10.0 %copy-start.5 = (f32[16,32,128]{2,1,0:T(8,128)S(1)}, f32[16,32,128]{2,1,0:T(8,128)}, u32[]{:S(2)}) copy-start(f32[16,32,128]{2,1,0:T(8,128)} %vy_ref.1) | copy-start | bytes 786436
  50.0 10.0 %copy-start.6 = (f32[16,32,128]{2,1,0:T(8,128)S(1)}, f32[16,32,128]{2,1,0:T(8,128)}, u32[]{:S(2)}) copy-start(f32[16,32,128]{2,1,0:T(8,128)} %vz_ref.1) | copy-start | bytes 786436
  50.1 6.4 %collective-permute-start.2 = (f32[2,16,16,128]{3,2,1,0:T(8,128)S(1)}, f32[2,16,16,128]{3,2,1,0:T(8,128)S(1)}, u32[]{:S(2)}, u32[]{:S(2)}) collective-permute-start(f32[2,16,16,128]{3,2,1,0:T(8,128)S(1)} %get-tuple-element.19), channel_id=1, source_target_pairs={{0,16},{16,32},{32,48},{48,64},{64,80},{80,96},{96,112},{112,128},... | collective-permute-start | bytes 786440 | tf_op jit(solution)/shard_map/ppermute | solution.py:546
  53.2 6.1 %collective-permute-start.3 = (f32[2,16,16,128]{3,2,1,0:T(8,128)S(1)}, f32[2,16,16,128]{3,2,1,0:T(8,128)S(1)}, u32[]{:S(2)}, u32[]{:S(2)}) collective-permute-start(f32[2,16,16,128]{3,2,1,0:T(8,128)S(1)} %get-tuple-element.20), channel_id=1, source_target_pairs={{16,0},{32,16},{48,32},{64,48},{80,64},{96,80},{112,96},{128,112},... | collective-permute-start | bytes 786440 | tf_op jit(solution)/shard_map/ppermute | solution.py:547
  54.0 6.1 %copy-start = (bf16[2,512,512]{2,1,0:T(8,128)(2,1)S(1)}, bf16[2,512,512]{2,1,0:T(8,128)(2,1)}, u32[]{:S(2)}) copy-start(bf16[2,512,512]{2,1,0:T(8,128)(2,1)} %constant.67.clone.fy_ref) | copy-start | bytes 3145732
  54.0 6.1 %copy-start.1 = (bf16[2,512,512]{2,1,0:T(8,128)(2,1)S(1)}, bf16[2,512,512]{2,1,0:T(8,128)(2,1)}, u32[]{:S(2)}) copy-start(bf16[2,512,512]{2,1,0:T(8,128)(2,1)} %constant.68.clone.gy_ref) | copy-start | bytes 3145732
  54.0 6.1 %copy-start.2 = (f32[3,32,8,128]{3,2,1,0:T(8,128)S(1)}, f32[3,32,8,128]{3,2,1,0:T(8,128)}, u32[]{:S(2)}) copy-start(f32[3,32,8,128]{3,2,1,0:T(8,128)} %constant.69.clone.yd_ref) | copy-start | bytes 1179652
  54.0 6.1 %copy-start.9 = (f32[5,16,128]{2,1,0:T(8,128)S(1)}, f32[5,16,128]{2,1,0:T(8,128)}, u32[]{:S(2)}) copy-start(f32[5,16,128]{2,1,0:T(8,128)} %constant.72.clone.xt_ref) | copy-start | bytes 122884

commit v2 on v1

--- a/solution.py
+++ b/solution.py
@@ -12,13 +12,14 @@
 time_step = 0.15
 reference_speed = 2.0
 absorption = 6.0
-highest = lax.Precision.HIGHEST
 MESH = pl.DeviceIdType.MESH
 
 NZ, NY, NX = 16, 512, 2048
 ROWS, COLS = 16, 16
 YB, XB = NY // ROWS, NX // COLS
-SLOTS = 8
+SLOTS, HALO = 8, 16
+VMEM_BYTES = 67043328
+TAPS, LABELS = 33, 12
 f32, bf16 = jnp.float32, jnp.bfloat16
 
 
@@ -199,13 +200,41 @@
 
 
 def step_kernel(
-    p_ref, vx_ref, vy_ref, vz_ref, b_ref, m_ref, dx_ref, dy_ref,
+    lab_hbm, p_hbm, vx_hbm, vy_hbm, vz_hbm, speed_hbm, density_hbm, taps_hbm, width_hbm,
+    fy_hbm, gy_hbm, yd_hbm, wx_hbm, ux_hbm, xt_hbm,
+    po_hbm, vxo_hbm, vyo_hbm, vzo_hbm,
+    row_out, row_in, col_out, col_in, bcol_out, bcol_in, brow_out, brow_in,
+    kappa, xb, xs, coef, lab, edge_out, edge_in, raw, across, edge_band, down, damp,
+    lab_ref, p_ref, vx_ref, vy_ref, vz_ref, speed_ref, density_ref, taps_ref, width_ref,
     fy_ref, gy_ref, yd_ref, wx_ref, ux_ref, xt_ref,
     po_ref, vxo_ref, vyo_ref, vzo_ref,
-    row_out, row_in, col_out, col_in, bcol_out, bcol_in, brow_out, brow_in,
-    kappa, xb, xs,
-    send_sem, recv_sem,
+    send_sem, recv_sem, load_sem, store_sem,
 ):
+    fetches = [
+        pltpu.make_async_copy(source, target, load_sem.at[n])
+        for n, (source, target) in enumerate(
+            [
+                (p_hbm, p_ref), (lab_hbm, lab_ref), (xt_hbm, xt_ref), (taps_hbm, taps_ref),
+                (width_hbm, width_ref), (fy_hbm, fy_ref), (wx_hbm, wx_ref),
+                (speed_hbm, speed_ref), (density_hbm, density_ref), (ux_hbm, ux_ref),
+                (gy_hbm, gy_ref), (vx_hbm, vx_ref), (yd_hbm, yd_ref), (vy_hbm, vy_ref),
+                (vz_hbm, vz_ref),
+            ]
+        )
+    ]
+    for fetch in fetches:
+        fetch.start()
+    writes = [
+        pltpu.make_async_copy(source, target, store_sem.at[n])
+        for n, (source, target) in enumerate(
+            [(vxo_ref, vxo_hbm), (vyo_ref, vyo_hbm), (vzo_ref, vzo_hbm), (po_ref, po_hbm)]
+        )
+    ]
+
+    def loaded(*numbers):
+        for n in numbers:
+            fetches[n].wait()
+
     r, c = lax.axis_index("row"), lax.axis_index("col")
     j, h = r // 2, r % 2
     q = h * COLS + c
@@ -297,7 +326,157 @@
     def pressure_planes(rows):
         store(row_out.at[0], rows, depth_forward(load(p_ref, rows)))
 
+    loaded(0)
     chunks(pressure_planes)
+
+    loaded(1)
+    for z in range(NZ):
+        lab[z, HALO : HALO + YB, :] = lab_ref[z].astype(f32)
+
+    def y_edges():
+        before, after = (r + ROWS - 1) % ROWS, (r + 1) % ROWS
+        return [
+            pltpu.make_async_remote_copy(
+                src_ref=lab.at[:, pl.ds(HALO, HALO), :],
+                dst_ref=lab.at[:, pl.ds(HALO + YB, HALO), :],
+                send_sem=send_sem.at[14], recv_sem=recv_sem.at[14],
+                device_id=(before, c), device_id_type=MESH,
+            ),
+            pltpu.make_async_remote_copy(
+                src_ref=lab.at[:, pl.ds(YB, HALO), :],
+                dst_ref=lab.at[:, pl.ds(0, HALO), :],
+                send_sem=send_sem.at[15], recv_sem=recv_sem.at[15],
+                device_id=(after, c), device_id_type=MESH,
+            ),
+        ]
+
+    def x_edges():
+        before, after = (c + COLS - 1) % COLS, (c + 1) % COLS
+        return [
+            pltpu.make_async_remote_copy(
+                src_ref=edge_out.at[0], dst_ref=edge_in.at[1],
+                send_sem=send_sem.at[16], recv_sem=recv_sem.at[16],
+                device_id=(r, before), device_id_type=MESH,
+            ),
+            pltpu.make_async_remote_copy(
+                src_ref=edge_out.at[1], dst_ref=edge_in.at[0],
+                send_sem=send_sem.at[17], recv_sem=recv_sem.at[17],
+                device_id=(r, after), device_id_type=MESH,
+            ),
+        ]
+
+    def ids(shape, dim):
+        return lax.broadcasted_iota(jnp.int32, shape, dim)
+
+    def banded(offset):
+        def tap(t, total):
+            return jnp.where(offset == t, taps_ref[t], total)
+
+        return lax.fori_loop(0, TAPS, tap, jnp.zeros(offset.shape, f32), unroll=3)
+
+    def fill_bands():
+        wide = (XB, XB)
+        band = banded(ids(wide, 0) - ids(wide, 1) + HALO)
+        none = jnp.zeros(wide, bf16)
+        for part, value in enumerate(halves(band)):
+            top_rows = jnp.concatenate([value, none], axis=1)
+            low_rows = jnp.concatenate([none, value], axis=1)
+            across[part] = jnp.concatenate([top_rows, low_rows], axis=0)
+        edge_band[0] = banded(ids(wide, 0) % HALO - ids(wide, 1))
+        edge_band[1] = banded(ids(wide, 0) % HALO - ids(wide, 1) + XB + HALO)
+        tall = (4 * YB, 8 * YB)
+        row, line = ids(tall, 0), ids(tall, 1)
+        offset = jnp.where(row // YB == line // (2 * YB), line % (2 * YB) - row % YB, -1)
+        for part, value in enumerate(halves(banded(offset))):
+            down[part] = value
+
+    def fill_damping():
+        def absorb(position, length, low_width, high_width):
+            size = position.shape
+            low_side = jnp.maximum(low_width - position, 0).astype(f32)
+            high_side = jnp.maximum(position - (length - 1 - high_width), 0).astype(f32)
+            low_side = low_side / jnp.full(size, low_width, jnp.int32).astype(f32)
+            high_side = high_side / jnp.full(size, high_width, jnp.int32).astype(f32)
+            low_side, high_side = low_side * low_side, high_side * high_side
+            total = low_side * low_side + high_side * high_side
+            return jnp.exp((-0.5 * time_step * absorption * reference_speed) * total)
+
+        damp[0:8] = absorb(c * XB + ids((8, XB), 1), NX, width_ref[0], width_ref[1])
+        damp[8:] = absorb(r * YB + ids((YB, XB), 0), NY, width_ref[2], width_ref[3])
+
+    def pack_edges():
+        wide = (XB, XB)
+        source, target = ids(wide, 0), ids(wide, 1)
+        total = None
+        for g in range(8):
+            here = target // HALO == g
+            first_lanes = here & (source == target % HALO)
+            last_lanes = here & (source == target % HALO + XB - HALO)
+            select = jnp.concatenate(
+                [jnp.where(first_lanes, 1.0, 0.0), jnp.where(last_lanes, 1.0, 0.0)], axis=1
+            ).astype(bf16)
+            part = mm(lab[2 * g : 2 * g + 2].reshape(XB, XB).astype(bf16), select)
+            total = part if total is None else total + part
+        edge_out[0] = total[:, :XB]
+        edge_out[1] = total[:, XB:]
+
+    def tables():
+        density = [jnp.full((8, XB), density_ref[n], f32) for n in range(LABELS)]
+        speed = [jnp.full((8, XB), speed_ref[n], f32) for n in range(LABELS)]
+        return [1.0 / d for d in density], [d * s * s for d, s in zip(density, speed)]
+
+    def look_up(label, table):
+        value = jnp.broadcast_to(table[0][None], label.shape)
+        for n in range(1, LABELS):
+            value = jnp.where(label == float(n), table[n][None], value)
+        return value
+
+    def fill_raw():
+        buoyancy_of, modulus_of = tables()
+
+        def plane(z, carry):
+            label = lab[z].reshape(8, 8, XB)
+            rows = pl.ds(pl.multiple_of(z * 2 * YB, 2 * YB), 2 * YB)
+            raw[rows, :XB] = look_up(label, buoyancy_of).reshape(2 * YB, XB)
+            raw[rows, XB:] = look_up(label, modulus_of).reshape(2 * YB, XB)
+            return carry
+
+        lax.fori_loop(0, NZ, plane, 0)
+
+    def smooth():
+        buoyancy_of, modulus_of = tables()
+        edges = [edge_in[0].reshape(16, 8, XB), edge_in[1].reshape(16, 8, XB)]
+        sides = [
+            halves(jnp.concatenate([look_up(e, t).reshape(XB, XB) for e in edges], axis=1))
+            for t in (buoyancy_of, modulus_of)
+        ]
+        group_of = ids((XB, XB), 0) // HALO
+
+        def quarter(i, carry):
+            rows = pl.ds(pl.multiple_of(i * 8 * YB, 8 * YB), 8 * YB)
+            high, low_part = halves(raw[rows, :])
+            main = mm(high, across[0]) + mm(low_part, across[0]) + mm(high, across[1])
+            parts = []
+            for g in range(2):
+                inside = group_of == 2 * i + g
+                parts.append(
+                    jnp.concatenate(
+                        [jnp.where(inside, edge_band[s], 0.0) for s in range(2)], axis=0
+                    )
+                )
+            high, low_part = halves(jnp.concatenate(parts, axis=1))
+            columns = []
+            for side_high, side_low in sides:
+                out = mm(side_high, high) + mm(side_low, high) + mm(side_high, low_part)
+                columns.append(jnp.concatenate([out[:, :XB], out[:, XB:]], axis=0))
+            high, low_part = halves(main + jnp.concatenate(columns, axis=1))
+            out = mm(down[0], high) + mm(down[0], low_part) + mm(down[1], high)
+            planes = pl.ds(i * 4, 4)
+            coef[0, planes] = out[:, :XB].reshape(4, YB, XB)
+            coef[1, planes] = out[:, XB:].reshape(4, YB, XB)
+            return carry
+
+        lax.fori_loop(0, 4, quarter, 0)
 
     lane_rows = lax.broadcasted_iota(jnp.int32, (SLOTS, XB), 0)
     slot = q * SLOTS + lane_rows
@@ -332,10 +511,16 @@
             kappa[g, kc] = 1.0 + v2 * np.float32(-1.0 / 6.0) * series
         return carry
 
+    loaded(2)
     lax.fori_loop(0, COLS, fill_kappa, 0)
 
     pl.semaphore_wait(barrier, ROWS - 1 + 2 * COLS - 1)
     send_row(0)
+    for edge in y_edges():
+        edge.start()
+    loaded(3, 4)
+    fill_bands()
+    fill_damping()
 
     def lines(ref, f):
         return ref[f].reshape(NY, XB)
@@ -426,10 +611,20 @@
                 half_general * (hr - lr) + own_imag * hi + first_flat * pltpu.roll(xr, 7, 0)
             )
 
+    loaded(5)
     arrived("row", 0)
     col_out[0] = row_product(fy_ref, [lines(row_in, 0)])[0].reshape(2 * COLS, 2 * SLOTS, XB)
     send_col(0)
 
+    for edge in y_edges():
+        edge.wait_recv()
+    pack_edges()
+    for edge in x_edges():
+        edge.start()
+    loaded(7, 8)
+    fill_raw()
+
+    loaded(6, 9)
     arrived("col", 0)
     spectrum = x_forward(0)
     re, im = spectrum[..., :XB] * kappa[...], spectrum[..., XB:] * kappa[...]
@@ -439,11 +634,16 @@
     x_inverse(jnp.concatenate([re, im], axis=-1), 1)
     send_bcol(1)
 
+    for edge in x_edges():
+        edge.wait_recv()
+    smooth()
+    loaded(10, 11, 12, 13, 14)
+
     arrived("bcol", 0)
     brow_out[0] = row_product(gy_ref, [lines(bcol_in, 0)])[0].reshape(ROWS, YB, XB)
     send_brow(0)
 
-    dx = dx_ref[0:8, :]
+    dx = damp[0:8]
 
     arrived("brow", 0)
 
@@ -451,13 +651,14 @@
         grad = depth_inverse(load(brow_in.at[0], rows))
         fresh = []
         for z in range(NZ):
-            change = time_step * b_ref[z, rows, :] * grad[z]
+            change = time_step * coef[0, z, rows, :] * grad[z]
             fresh.append(dx * (dx * vx_ref[z, rows, :] - change))
         store(vxo_ref, rows, fresh)
         store(row_out.at[1], rows, depth_forward(fresh))
 
     chunks(update_x)
     send_row(1)
+    writes[0].start()
 
     arrived("bcol", 1)
     flow = lines(bcol_in, 1)
@@ -475,16 +676,17 @@
 
     def update_y(rows):
         grad = depth_inverse(load(brow_in.at[1], rows))
-        dy = dy_ref[rows, :]
+        dy = damp[pl.ds(pl.multiple_of(rows.start + 8, 8), 8), :]
         fresh = []
         for z in range(NZ):
-            change = time_step * b_ref[z, rows, :] * grad[z]
+            change = time_step * coef[0, z, rows, :] * grad[z]
             fresh.append(dy * (dy * vy_ref[z, rows, :] - change))
         store(vyo_ref, rows, fresh)
         store(row_out.at[2], rows, depth_forward(fresh))
 
     chunks(update_y)
     send_row(2)
+    writes[1].start()
 
     arrived("brow", 2)
 
@@ -492,12 +694,13 @@
         grad = depth_inverse(depth_derivative(load(brow_in.at[2], rows), 1))
         fresh = []
         for z in range(NZ):
-            fresh.append(vz_ref[z, rows, :] - time_step * b_ref[z, rows, :] * grad[z])
+            fresh.append(vz_ref[z, rows, :] - time_step * coef[0, z, rows, :] * grad[z])
         store(vzo_ref, rows, fresh)
         store(row_out.at[3], rows, depth_derivative(depth_forward(fresh), -1))
 
     chunks(update_z)
     send_row(3)
+    writes[2].start()
 
     arrived("row", 2)
     arrived("row", 3)
@@ -524,107 +727,96 @@
 
     def update_p(rows):
         divergence = depth_inverse(load(brow_in.at[3], rows))
-        both = dx * dy_ref[rows, :]
+        both = dx * damp[pl.ds(pl.multiple_of(rows.start + 8, 8), 8), :]
         for z in range(NZ):
-            change = time_step * m_ref[z, rows, :] * divergence[z]
+            change = time_step * coef[1, z, rows, :] * divergence[z]
             po_ref[z, rows, :] = both * (both * p_ref[z, rows, :] - change)
 
     chunks(update_p)
+    writes[3].start()
 
     for kind, number in (("row", 4), ("col", 3), ("bcol", 3), ("brow", 4)):
         for f in range(number):
             all_of(kind, f).wait_send()
-
-
-def extended(array, sides, width):
-    for axis, dim in sides:
-        size, length = (lax.axis_size(axis), array.shape[dim])
-        up = [(i, (i + 1) % size) for i in range(size)]
-        down = [(j, i) for i, j in up]
-        last = lax.slice_in_dim(array, length - width, length, axis=dim)
-        initial = lax.slice_in_dim(array, 0, width, axis=dim)
-        before = lax.ppermute(last, axis, up)
-        after = lax.ppermute(initial, axis, down)
-        array = jnp.concatenate([before, array, after], axis=dim)
-    return array
-
-
-def band_matrix(filter_taps, extent):
-    tap_count = filter_taps.shape[0]
-    offset = (
-        jnp.arange(extent + tap_count - 1, dtype=jnp.int32)[:, None]
-        - jnp.arange(extent, dtype=jnp.int32)[None, :]
-    )
-    selected = offset[:, :, None] == jnp.arange(tap_count, dtype=jnp.int32)[None, None, :]
-    return jnp.sum(jnp.where(selected, filter_taps[None, None, :], 0.0), axis=2)
-
-
-def absorber(position, length, low_width, high_width):
-    low_part = jnp.maximum(low_width - position, 0).astype(f32) / low_width.astype(f32)
-    high_part = jnp.maximum(position - (length - 1 - high_width), 0).astype(
-        f32
-    ) / high_width.astype(f32)
-    damping = absorption * reference_speed * (low_part**4 + high_part**4)
-    return jnp.exp(-0.5 * time_step * damping)
+    for edge in y_edges() + x_edges():
+        edge.wait_send()
+    for write in writes:
+        write.wait()
+
+
+def write_kernel(a, b, c, d, a_out, b_out, c_out, d_out, held, in_sem, out_sem):
+    arrays = ((a, a_out), (b, b_out), (c, c_out), (d, d_out))
+    loads = [pltpu.make_async_copy(x, held.at[n], in_sem.at[n]) for n, (x, _) in enumerate(arrays)]
+    stores = [pltpu.make_async_copy(held.at[n], y, out_sem.at[n]) for n, (_, y) in enumerate(arrays)]
+    for load in loads:
+        load.start()
+    for load, store in zip(loads, stores):
+        load.wait()
+        store.start()
+    for store in stores:
+        store.wait()
 
 
 def on_device(
     labels, pressure, velocity_x, velocity_y, velocity_z,
     speed_table, density_table, filter_taps, layer_width,
 ):
-    planes, height, breadth = pressure.shape
-    buoyancy_of = 1.0 / density_table
-    modulus_of = density_table * speed_table * speed_table
-    buoyancy = jnp.zeros(pressure.shape, f32)
-    modulus = jnp.zeros(pressure.shape, f32)
-    for label_id in range(speed_table.shape[0]):
-        matches = labels == label_id
-        buoyancy = jnp.where(matches, buoyancy_of[label_id], buoyancy)
-        modulus = jnp.where(matches, modulus_of[label_id], modulus)
-    coefficients = jnp.stack([buoyancy, modulus])
-    reach = filter_taps.shape[0] // 2
-    across = band_matrix(filter_taps, breadth)
-    downward = band_matrix(filter_taps, height)
-    padded = extended(coefficients, (("col", 3),), reach)
-    smoothed = jnp.einsum("fzyj,ji->fzyi", padded, across, precision=highest)
-    padded = extended(smoothed, (("row", 2),), reach)
-    smoothed = jnp.einsum("fzjx,jy->fzyx", padded, downward, precision=highest)
-    buoyancy = smoothed[0]
-    modulus = smoothed[1]
-    column_ids = lax.axis_index("col") * breadth + jnp.arange(breadth, dtype=jnp.int32)
-    row_ids = lax.axis_index("row") * height + jnp.arange(height, dtype=jnp.int32)
-    damp_x = absorber(column_ids, NX, layer_width[0], layer_width[1])
-    damp_y = absorber(row_ids, NY, layer_width[2], layer_width[3])
-    damp_x = jnp.broadcast_to(damp_x[None, :], (8, breadth))
-    damp_y = jnp.broadcast_to(damp_y[:, None], (height, breadth))
-
     fy, gy, yd = row_tables()
     wx, ux, xt = column_tables()
     brick = jax.ShapeDtypeStruct(pressure.shape, f32)
     row_buffer = lambda n: pltpu.VMEM((n, ROWS, YB, XB), f32)
     col_buffer = lambda n: pltpu.VMEM((n, 2 * COLS, 2 * SLOTS, XB), f32)
-    return pl.pallas_call(
+    results = pl.pallas_call(
         step_kernel,
         out_shape=(brick,) * 4,
-        in_specs=[pl.BlockSpec(memory_space=pltpu.VMEM)] * 14,
-        out_specs=(pl.BlockSpec(memory_space=pltpu.VMEM),) * 4,
+        in_specs=[pl.BlockSpec(memory_space=pl.ANY)] * 15,
+        out_specs=(pl.BlockSpec(memory_space=pl.ANY),) * 4,
         scratch_shapes=[
             row_buffer(4), row_buffer(4), col_buffer(3), col_buffer(3),
             col_buffer(3), col_buffer(3), row_buffer(4), row_buffer(4),
             pltpu.VMEM((3, COLS, SLOTS, XB), f32),
             pltpu.VMEM((3, 2, COLS, SLOTS, XB), f32),
             pltpu.VMEM((1, 3, COLS, SLOTS, 2 * XB), f32),
-            pltpu.SemaphoreType.DMA((14,)),
-            pltpu.SemaphoreType.DMA((14,)),
+            pltpu.VMEM((2, NZ, YB, XB), f32),
+            pltpu.VMEM((NZ, 2 * YB, XB), f32),
+            pltpu.VMEM((2, XB, XB), f32),
+            pltpu.VMEM((2, XB, XB), f32),
+            pltpu.VMEM((NZ * 2 * YB, 2 * XB), f32),
+            pltpu.VMEM((2, 2 * XB, 2 * XB), bf16),
+            pltpu.VMEM((2, XB, XB), f32),
+            pltpu.VMEM((2, 4 * YB, 8 * YB), bf16),
+            pltpu.VMEM((8 + YB, XB), f32),
+            pltpu.VMEM(labels.shape, jnp.int32),
+            *[pltpu.VMEM(pressure.shape, f32)] * 4,
+            pltpu.SMEM((LABELS,), f32), pltpu.SMEM((LABELS,), f32),
+            pltpu.SMEM((TAPS,), f32), pltpu.SMEM((4,), jnp.int32),
+            *[pltpu.VMEM(t.shape, t.dtype) for t in (fy, gy, yd, wx, ux, xt)],
+            *[pltpu.VMEM(pressure.shape, f32)] * 4,
+            pltpu.SemaphoreType.DMA((18,)),
+            pltpu.SemaphoreType.DMA((18,)),
+            pltpu.SemaphoreType.DMA((15,)),
+            pltpu.SemaphoreType.DMA((4,)),
         ],
         compiler_params=pltpu.CompilerParams(
-            collective_id=0, has_side_effects=True, vmem_limit_bytes=48 * 1024 * 1024
+            collective_id=0, has_side_effects=True, vmem_limit_bytes=VMEM_BYTES
         ),
     )(
-        pressure, velocity_x, velocity_y, velocity_z, buoyancy, modulus, damp_x, damp_y,
+        labels, pressure, velocity_x, velocity_y, velocity_z,
+        speed_table, density_table, filter_taps, layer_width,
         jnp.asarray(fy), jnp.asarray(gy), jnp.asarray(yd),
         jnp.asarray(wx), jnp.asarray(ux), jnp.asarray(xt),
     )
+    return pl.pallas_call(
+        write_kernel,
+        out_shape=(brick,) * 4,
+        in_specs=[pl.BlockSpec(memory_space=pl.ANY)] * 4,
+        out_specs=(pl.BlockSpec(memory_space=pl.ANY),) * 4,
+        scratch_shapes=[
+            pltpu.VMEM((4,) + pressure.shape, f32),
+            pltpu.SemaphoreType.DMA((4,)), pltpu.SemaphoreType.DMA((4,)),
+        ],
+        compiler_params=pltpu.CompilerParams(vmem_limit_bytes=VMEM_BYTES),
+    )(*results)
 
 
 def solution(mesh):

time: 154 us -> 98.2 us (0.64)
  other arithmetic: 19.7 us -> 0 us
  waiting for transfers between devices: 19.6 us -> 0 us
  starting transfers between devices: 12.1 us -> 0 us
  Pallas kernels: 91.1 us -> 97.4 us
  local copies, waits for them, and re-layouts: 5.03 us -> 0 us
  between operations: 4.79 us -> 0.64 us
  matrix products: 1.76 us -> 0 us
    ppermute x4 -> x0, waiting for transfers between devices: 19.6 us -> none  [the longest x2 13.4 us: extended(): before = lax.ppermute(last, axis, up)]
    another operation x3 -> x0, other arithmetic: 17.2 us -> none  [on_device(): coefficients = jnp.stack([buoyancy, modulus])]
    ppermute x4 -> x0, starting transfers between devices: 12.1 us -> none  [the longest x2 6.71 us: extended(): before = lax.ppermute(last, axis, up)]
    pallas_call x1, Pallas kernels: 91.1 us -> 95.4 us  [on_device(): pl.pallas_call(step_kernel, out_shape=(brick,) * 4, in_specs=[pl.BlockSpe...]
    unnamed x28 -> x0, local copies, waits for them, and re-layouts: 2.88 us -> none
    slice x4 -> x0, local copies, waits for them, and re-layouts: 2.03 us -> none  [the longest x1 0.7 us: on_device(): buoyancy = jnp.where(matches, buoyancy_of[label_id], buoyancy)]
    pallas_call x0 -> x1, Pallas kernels: none -> 1.98 us  [on_device(): pl.pallas_call(write_kernel, out_shape=(brick,) * 4, in_specs=[pl.BlockSp...]
    dot_general x2 -> x0, matrix products: 1.76 us -> none  [the longest x1 1.14 us: on_device(): smoothed = jnp.einsum('fzyj,ji->fzyi', padded, across, precision=highest)]
  transfers between devices with their start and end apart: 4 -> 0, of which waited for: 4 -> 0; matrix products, arithmetic and copies ran while one was open for 2% -> 0% of each run, Pallas kernels for 0% -> 0%
where the time goes in v2:
time: 98.2 us; the launch traced here: 98 us
  Pallas kernels  97.4 us (99%)
    pallas_call x1, Pallas kernels, on_device(): pl.pallas_call(step_kernel, out_shape=(brick,) * 4, in_specs=[pl.BlockSpe...  95.4 us
    pallas_call x1, Pallas kernels, on_device(): pl.pallas_call(write_kernel, out_shape=(brick,) * 4, in_specs=[pl.BlockSp...  1.98 us

profile of v2, /device:TPU:1, one launch (start us, length us, event | category | flops | bytes accessed | tf_op | source)
XLA Modules:
  0.0 98.0 jit_solution(9685728249573245036)
XLA Ops:
  0.6 95.4 %shard_map.174 = (f32[16,32,128]{2,1,0:T(8,128)}, f32[16,32,128]{2,1,0:T(8,128)}, f32[16,32,128]{2,1,0:T(8,128)}, f32[16,32,128]{2,1,0:T(8,128)}) custom-call(s32[16,32,128]{2,1,0:T(8,128)} %lab_hbm.1, f32[16,32,128]{2,1,0:T(8,128)} %p_hbm.1, f32[16,32,128]{2,1,0:T(8,128)} %vx_hbm.1, f32[16,32,128]{2,1,0:T(8,128)} %vy_hbm.1, f32[16,32,128]{2,1,0:T(8,128)} %vz_hbm.1, ...), custom_call_target="tpu_custom_call" | custom-call | tf_op jit(solution)/shard_map/pallas_call | solution.py:769
  96.1 2.0 %shard_map.175 = (f32[16,32,128]{2,1,0:T(8,128)}, f32[16,32,128]{2,1,0:T(8,128)}, f32[16,32,128]{2,1,0:T(8,128)}, f32[16,32,128]{2,1,0:T(8,128)}) custom-call(f32[16,32,128]{2,1,0:T(8,128)} %get-tuple-element.8.a, f32[16,32,128]{2,1,0:T(8,128)} %get-tuple-element.9.b, f32[16,32,128]{2,1,0:T(8,128)} %get-tuple-element.10.c, f32[16,32,128]{2,1,0:T(8,128)} %get-tuple-element.11.d), custom_call_target="tpu_custom_call" | custom-call | tf_op jit(solution)/shard_map/pallas_call | solution.py:809

commit v3 on v2

--- a/solution.py
+++ b/solution.py
@@ -210,6 +210,63 @@
     po_ref, vxo_ref, vyo_ref, vzo_ref,
     send_sem, recv_sem, load_sem, store_sem,
 ):
+    writes = [
+        pltpu.make_async_copy(source, target, store_sem.at[n])
+        for n, (source, target) in enumerate(
+            [(vxo_ref, vxo_hbm), (vyo_ref, vyo_hbm), (vzo_ref, vzo_hbm), (po_ref, po_hbm)]
+        )
+    ]
+
+    def loaded(*numbers):
+        for n in numbers:
+            fetches[n].wait()
+
+    r, c = lax.axis_index("row"), lax.axis_index("col")
+    j, h = r // 2, r % 2
+    q = h * COLS + c
+
+    barrier = pltpu.get_barrier_semaphore()
+
+    x_low, y_chip, core = r // 8, (r // 2) % 4, r % 2
+    z_chip, x_high = c // 2, c % 2
+
+    def pick(i, values):
+        value = jnp.int32(values[0])
+        for n in range(1, len(values)):
+            value = jnp.where(i == n, jnp.int32(values[n]), value)
+        return value
+
+    def row_partner(i, other):
+        x = (x_low + pick(i, (1, 0, 1, 1, 0, 0, 1, 0))) % 2
+        y = (y_chip + pick(i, (2, 2, 1, 3, 1, 3, 0, 0))) % 4
+        return (x * 4 + y) * 2 + (core + other) % 2
+
+    def plane_partner(i, other):
+        z = (z_chip + pick(i, (4, 3, 5, 4, 2, 6, 3, 5, 1, 7, 2, 6, 0, 1, 7, 0))) % 8
+        x = (x_high + pick(i, (1, 1, 1, 0, 1, 1, 0, 0, 1, 1, 0, 0, 1, 0, 0, 0))) % 2
+        return (core + other) % 2 * COLS + z * 2 + x
+
+    def each_partner(partner, classes, body):
+        def step(i, carry):
+            body(partner(i, 0))
+            body(partner(i, 1))
+            return carry
+
+        lax.fori_loop(0, classes - 1, step, 0)
+        body(partner(classes - 1, 1))
+
+    def row_device(t):
+        return (t, c)
+
+    def plane_device(t):
+        return (2 * j + t // COLS, t % COLS)
+
+    def greet(device):
+        pl.semaphore_signal(barrier, inc=1, device_id=device, device_id_type=MESH)
+
+    each_partner(plane_partner, COLS, lambda t: greet(plane_device(t)))
+    each_partner(row_partner, ROWS // 2, lambda t: greet(row_device(t)))
+
     fetches = [
         pltpu.make_async_copy(source, target, load_sem.at[n])
         for n, (source, target) in enumerate(
@@ -224,59 +281,21 @@
     ]
     for fetch in fetches:
         fetch.start()
-    writes = [
-        pltpu.make_async_copy(source, target, store_sem.at[n])
-        for n, (source, target) in enumerate(
-            [(vxo_ref, vxo_hbm), (vyo_ref, vyo_hbm), (vzo_ref, vzo_hbm), (po_ref, po_hbm)]
-        )
-    ]
-
-    def loaded(*numbers):
-        for n in numbers:
-            fetches[n].wait()
-
-    r, c = lax.axis_index("row"), lax.axis_index("col")
-    j, h = r // 2, r % 2
-    q = h * COLS + c
-
-    barrier = pltpu.get_barrier_semaphore()
-
-    def greet_row(i, carry):
-        pl.semaphore_signal(barrier, inc=1, device_id=((r + i) % ROWS, c), device_id_type=MESH)
-        return carry
-
-    def greet_plane(i, carry):
-        t = (q + i) % (2 * COLS)
-        pl.semaphore_signal(
-            barrier, inc=1, device_id=(2 * j + t // COLS, t % COLS), device_id_type=MESH
-        )
-        return carry
-
-    lax.fori_loop(1, ROWS, greet_row, 0)
-    lax.fori_loop(1, 2 * COLS, greet_plane, 0)
-
-    def row_copy(src, dst, sem, i):
-        t = (r + i) % ROWS
-        return pltpu.make_async_remote_copy(
-            src_ref=src.at[t], dst_ref=dst.at[r], send_sem=send_sem.at[sem],
-            recv_sem=recv_sem.at[sem], device_id=(t, c), device_id_type=MESH,
-        )
-
-    def plane_copy(src, dst, sem, i):
-        t = (q + i) % (2 * COLS)
-        return pltpu.make_async_remote_copy(
-            src_ref=src.at[t], dst_ref=dst.at[q], send_sem=send_sem.at[sem],
-            recv_sem=recv_sem.at[sem], device_id=(2 * j + t // COLS, t % COLS),
-            device_id_type=MESH,
-        )
-
-    def start_all(copy_of, src, dst, sem, count, own):
-        def body(i, carry):
-            copy_of(src, dst, sem, i).start()
-            return carry
-
-        lax.fori_loop(1, count, body, 0)
+    def start_all(src, dst, sem, partner, classes, device_of, own):
+        def start(t):
+            pltpu.make_async_remote_copy(
+                src_ref=src.at[t], dst_ref=dst.at[own], send_sem=send_sem.at[sem],
+                recv_sem=recv_sem.at[sem], device_id=device_of(t), device_id_type=MESH,
+            ).start()
+
+        each_partner(partner, classes, start)
         dst[own] = src[own]
+
+    def row_all(src, dst, sem):
+        start_all(src, dst, sem, row_partner, ROWS // 2, row_device, r)
+
+    def plane_all(src, dst, sem):
+        start_all(src, dst, sem, plane_partner, COLS, plane_device, q)
 
     def whole(src, dst, sem, count):
         span = pl.ds(0, count - 1)
@@ -286,16 +305,16 @@
         )
 
     def send_row(f):
-        start_all(row_copy, row_out.at[f], row_in.at[f], f, ROWS, r)
+        row_all(row_out.at[f], row_in.at[f], f)
 
     def send_col(f):
-        start_all(plane_copy, col_out.at[f], col_in.at[f], 4 + f, 2 * COLS, q)
+        plane_all(col_out.at[f], col_in.at[f], 4 + f)
 
     def send_bcol(f):
-        start_all(plane_copy, bcol_out.at[f], bcol_in.at[f], 7 + f, 2 * COLS, q)
+        plane_all(bcol_out.at[f], bcol_in.at[f], 7 + f)
 
     def send_brow(f):
-        start_all(row_copy, brow_out.at[f], brow_in.at[f], 10 + f, ROWS, r)
+        row_all(brow_out.at[f], brow_in.at[f], 10 + f)
 
     def all_of(kind, f):
         src, dst, base, count = {
@@ -328,6 +347,8 @@
 
     loaded(0)
     chunks(pressure_planes)
+    pl.semaphore_wait(barrier, ROWS - 1 + 2 * COLS - 1)
+    send_row(0)
 
     loaded(1)
     for z in range(NZ):
@@ -514,8 +535,6 @@
     loaded(2)
     lax.fori_loop(0, COLS, fill_kappa, 0)
 
-    pl.semaphore_wait(barrier, ROWS - 1 + 2 * COLS - 1)
-    send_row(0)
     for edge in y_edges():
         edge.start()
     loaded(3, 4)

time: 98.2 us -> 91.7 us (0.934)
  Pallas kernels: 97.4 us -> 91 us
    pallas_call x1, Pallas kernels: 95.4 us -> 89 us  [on_device(): pl.pallas_call(step_kernel, out_shape=(brick,) * 4, in_specs=[pl.BlockSpe...]
where the time goes in v3:
time: 91.7 us; the launch traced here: 91.6 us
  Pallas kernels  91 us (99%)
    pallas_call x1, Pallas kernels, on_device(): pl.pallas_call(step_kernel, out_shape=(brick,) * 4, in_specs=[pl.BlockSpe...  89 us
    pallas_call x1, Pallas kernels, on_device(): pl.pallas_call(write_kernel, out_shape=(brick,) * 4, in_specs=[pl.BlockSp...  1.98 us

profile of v3, /device:TPU:1, one launch (start us, length us, event | category | flops | bytes accessed | tf_op | source)
XLA Modules:
  0.0 91.6 jit_solution(8638996798420930609)
XLA Ops:
  0.6 89.0 %shard_map.174 = (f32[16,32,128]{2,1,0:T(8,128)}, f32[16,32,128]{2,1,0:T(8,128)}, f32[16,32,128]{2,1,0:T(8,128)}, f32[16,32,128]{2,1,0:T(8,128)}) custom-call(s32[16,32,128]{2,1,0:T(8,128)} %lab_hbm.1, f32[16,32,128]{2,1,0:T(8,128)} %p_hbm.1, f32[16,32,128]{2,1,0:T(8,128)} %vx_hbm.1, f32[16,32,128]{2,1,0:T(8,128)} %vy_hbm.1, f32[16,32,128]{2,1,0:T(8,128)} %vz_hbm.1, ...), custom_call_target="tpu_custom_call" | custom-call | tf_op jit(solution)/shard_map/pallas_call | solution.py:788
  89.7 2.0 %shard_map.175 = (f32[16,32,128]{2,1,0:T(8,128)}, f32[16,32,128]{2,1,0:T(8,128)}, f32[16,32,128]{2,1,0:T(8,128)}, f32[16,32,128]{2,1,0:T(8,128)}) custom-call(f32[16,32,128]{2,1,0:T(8,128)} %get-tuple-element.8.a, f32[16,32,128]{2,1,0:T(8,128)} %get-tuple-element.9.b, f32[16,32,128]{2,1,0:T(8,128)} %get-tuple-element.10.c, f32[16,32,128]{2,1,0:T(8,128)} %get-tuple-element.11.d), custom_call_target="tpu_custom_call" | custom-call | tf_op jit(solution)/shard_map/pallas_call | solution.py:828

commit v4 on v3

--- a/solution.py
+++ b/solution.py
@@ -17,7 +17,8 @@
 NZ, NY, NX = 16, 512, 2048
 ROWS, COLS = 16, 16
 YB, XB = NY // ROWS, NX // COLS
-SLOTS, HALO = 8, 16
+SLOTS, HALO = 4, 16
+CHUNK = 2 * COLS * SLOTS
 VMEM_BYTES = 67043328
 TAPS, LABELS = 33, 12
 f32, bf16 = jnp.float32, jnp.bfloat16
@@ -35,19 +36,22 @@
     angle = 2.0 * np.pi * ((slot[:, None] * y[None, :]) % NY) / NY
     real, imag = np.cos(angle), -np.sin(angle)
     imag[0] = np.where(y % 2 == 0, 1.0, -1.0)
-    order = lambda t: t.reshape(NY // 2 // SLOTS, SLOTS, NY)
-    forward = np.stack([order(real), order(imag)], axis=1).reshape(NY, NY)
-    weight = np.where(slot == 0, 1.0, 2.0) / NY
-    inverse = np.stack([order(real * weight[:, None]), order(imag * weight[:, None])], axis=1)
-    inverse = inverse.reshape(NY, NY).T
+
+    def order(a, b):
+        pair = [t.reshape((2 * 2 * COLS, SLOTS) + t.shape[1:]) for t in (a, b)]
+        return np.stack(pair, axis=1)
+
+    forward = order(real, imag).reshape(NY, NY)
+    weight = np.where(slot == 0, 1.0, 2.0)[:, None] / NY
+    inverse = order(real * weight, imag * weight).reshape(NY, NY).T
     wave = 2.0 * np.pi * slot / NY
     same = -wave * np.sin(0.5 * wave)
     cross = wave * np.cos(0.5 * wave)
     same_imag = same.copy()
     same_imag[0] = -np.pi
-    wide = lambda v: np.broadcast_to(v.reshape(-1, SLOTS, 1), (NY // 2 // SLOTS, SLOTS, XB))
-    derivative = np.stack([wide(same), wide(same_imag), wide(cross)]).astype(np.float32)
-    return split_table(forward), split_table(inverse), derivative
+    tables = [order(same, same_imag), order(-cross, cross)]
+    wide = [np.broadcast_to(t.reshape(-1, 2 * SLOTS, 1), (NY // 8, 8, XB)) for t in tables]
+    return split_table(forward), split_table(inverse), np.stack(wide).astype(np.float32)
 
 
 def column_tables():
@@ -307,26 +311,26 @@
     def send_row(f):
         row_all(row_out.at[f], row_in.at[f], f)
 
-    def send_col(f):
-        plane_all(col_out.at[f], col_in.at[f], 4 + f)
-
-    def send_bcol(f):
-        plane_all(bcol_out.at[f], bcol_in.at[f], 7 + f)
+    def send_col(f, u):
+        plane_all(col_out.at[f, u], col_in.at[f, u], 4 + 2 * f + u)
+
+    def send_bcol(f, u):
+        plane_all(bcol_out.at[f, u], bcol_in.at[f, u], 10 + 2 * f + u)
 
     def send_brow(f):
-        row_all(brow_out.at[f], brow_in.at[f], 10 + f)
-
-    def all_of(kind, f):
-        src, dst, base, count = {
-            "row": (row_out, row_in, 0, ROWS),
-            "col": (col_out, col_in, 4, 2 * COLS),
-            "bcol": (bcol_out, bcol_in, 7, 2 * COLS),
-            "brow": (brow_out, brow_in, 10, ROWS),
-        }[kind]
-        return whole(src.at[f], dst.at[f], base + f, count)
-
-    def arrived(kind, f):
-        all_of(kind, f).wait_recv()
+        row_all(brow_out.at[f], brow_in.at[f], 16 + f)
+
+    def all_of(kind, f, u=None):
+        if kind == "row":
+            return whole(row_out.at[f], row_in.at[f], f, ROWS)
+        if kind == "brow":
+            return whole(brow_out.at[f], brow_in.at[f], 16 + f, ROWS)
+        if kind == "col":
+            return whole(col_out.at[f, u], col_in.at[f, u], 4 + 2 * f + u, 2 * COLS)
+        return whole(bcol_out.at[f, u], bcol_in.at[f, u], 10 + 2 * f + u, 2 * COLS)
+
+    def arrived(kind, f, u=None):
+        all_of(kind, f, u).wait_recv()
 
     def load(ref, rows):
         return [ref[z, rows, :] for z in range(NZ)]
@@ -360,13 +364,13 @@
             pltpu.make_async_remote_copy(
                 src_ref=lab.at[:, pl.ds(HALO, HALO), :],
                 dst_ref=lab.at[:, pl.ds(HALO + YB, HALO), :],
-                send_sem=send_sem.at[14], recv_sem=recv_sem.at[14],
+                send_sem=send_sem.at[20], recv_sem=recv_sem.at[20],
                 device_id=(before, c), device_id_type=MESH,
             ),
             pltpu.make_async_remote_copy(
                 src_ref=lab.at[:, pl.ds(YB, HALO), :],
                 dst_ref=lab.at[:, pl.ds(0, HALO), :],
-                send_sem=send_sem.at[15], recv_sem=recv_sem.at[15],
+                send_sem=send_sem.at[21], recv_sem=recv_sem.at[21],
                 device_id=(after, c), device_id_type=MESH,
             ),
         ]
@@ -376,12 +380,12 @@
         return [
             pltpu.make_async_remote_copy(
                 src_ref=edge_out.at[0], dst_ref=edge_in.at[1],
-                send_sem=send_sem.at[16], recv_sem=recv_sem.at[16],
+                send_sem=send_sem.at[22], recv_sem=recv_sem.at[22],
                 device_id=(r, before), device_id_type=MESH,
             ),
             pltpu.make_async_remote_copy(
                 src_ref=edge_out.at[1], dst_ref=edge_in.at[0],
-                send_sem=send_sem.at[17], recv_sem=recv_sem.at[17],
+                send_sem=send_sem.at[23], recv_sem=recv_sem.at[23],
                 device_id=(r, after), device_id_type=MESH,
             ),
         ]
@@ -499,31 +503,35 @@
 
         lax.fori_loop(0, 4, quarter, 0)
 
-    lane_rows = lax.broadcasted_iota(jnp.int32, (SLOTS, XB), 0)
-    slot = q * SLOTS + lane_rows
-    one, zero = jnp.ones((SLOTS, XB), f32), jnp.zeros((SLOTS, XB), f32)
-    first = jnp.where(slot == 0, one, zero)
-    flat = jnp.where(jnp.full((SLOTS, XB), j, jnp.int32) == 0, one, zero)
-    general = (1.0 - first) * (1.0 - flat)
-    half_general = 0.5 * general
-    first_deep = first * (1.0 - flat)
-    first_flat = first * flat
-    rest_flat = flat * (1.0 - first)
-    own_imag = first_deep + rest_flat
-    not_first = 1.0 - first
-    not_flat = 1.0 - flat
+    tile_rows = lax.broadcasted_iota(jnp.int32, (8, XB), 0)
+    one, zero = jnp.ones((8, XB), f32), jnp.zeros((8, XB), f32)
+    top = jnp.where(tile_rows < SLOTS, one, zero)
+    bottom = 1.0 - top
+    flat = jnp.where(jnp.full((8, XB), j, jnp.int32) == 0, one, zero)
+    deep = 1.0 - flat
+
+    def slot_of(u):
+        return u * CHUNK + q * SLOTS + tile_rows % SLOTS
+
+    def first_of(u):
+        return jnp.where(slot_of(u) == 0, one, zero)
+
+    def turned(value):
+        return pltpu.roll(value, SLOTS, 0)
 
     pi2 = np.float32(math.pi * math.pi)
-    ky = slot.astype(f32) * np.float32(2.0 * math.pi / NY)
-    kz = jnp.full((SLOTS, XB), j, jnp.int32).astype(f32) * np.float32(2.0 * math.pi / NZ)
-    low = ky * ky + kz * kz
-    top = low + pi2 * (first_deep + flat)
-    extra = pi2 + jnp.where(lane_rows == 0, zero, pi2 * one)
+    kz = jnp.full((8, XB), j, jnp.int32).astype(f32) * np.float32(2.0 * math.pi / NZ)
+
+    def square_of(u):
+        ky = slot_of(u).astype(f32) * np.float32(2.0 * math.pi / NY)
+        return ky * ky + kz * kz + pi2 * bottom * (first_of(u) * deep + flat)
+
+    squares = (square_of(0), pi2 + pi2 * bottom, square_of(1))
     scale = np.float32((0.5 * reference_speed * time_step) ** 2)
 
     def fill_kappa(kc, carry):
         kx2 = xt_ref[2, pl.ds(kc, 1), :]
-        for g, part in enumerate((low, top, extra)):
+        for g, part in enumerate(squares):
             v2 = scale * (kx2 + part)
             series = 1.0 + v2 * np.float32(-1.0 / 110.0)
             series = 1.0 + v2 * np.float32(-1.0 / 72.0) * series
@@ -543,6 +551,11 @@
 
     def lines(ref, f):
         return ref[f].reshape(NY, XB)
+
+    def put_col(f, value):
+        col_out[f] = value.reshape(2, 2 * COLS, 2 * SLOTS, XB)
+        send_col(f, 0)
+        send_col(f, 1)
 
     def row_product(table, values):
         parts = [halves(v) for v in values]
@@ -557,25 +570,28 @@
         return [result[:, :XB], result[:, XB:]]
 
     def y_derivative(value, sign):
-        parts = value.reshape(NY // 2 // SLOTS, 2, SLOTS, XB)
-        re, im = parts[:, 0], parts[:, 1]
-        same, same_imag, cross = yd_ref[0], yd_ref[1], yd_ref[2]
-        if sign > 0:
-            out = [re * same - im * cross, im * same_imag + re * cross]
-        else:
-            out = [-(re * same + im * cross), re * cross - im * same_imag]
-        return jnp.stack(out, axis=1).reshape(NY, XB)
-
-    def x_forward(f):
+        tiles = value.reshape(NY // 8, 8, XB)
+        same = tiles * yd_ref[0]
+        cross = pltpu.roll(tiles, SLOTS, 1) * yd_ref[1]
+        return (cross + same if sign > 0 else cross - same).reshape(NY, XB)
+
+    def x_forward(f, u):
+        first, groups = first_of(u), 2 - u
+        general = (1.0 - first) * deep
+        rest = (1.0 - first) * flat
+        lone = first * deep
+        re_r, re_turned_r = top + bottom * lone, bottom * general
+        re_i, re_turned_i = bottom * general, bottom * flat - top * general
+        im_r, im_turned_r = -bottom * general, top * (general + rest)
+        im_i, im_turned_i = top * general + lone + bottom * rest, bottom * general
         for n in range(COLS):
-            rr, ri = col_in[f, n, 0:8, :], col_in[f, n, 8:16, :]
-            ir, ii = col_in[f, COLS + n, 0:8, :], col_in[f, COLS + n, 8:16, :]
-            xb[0, 0, n] = rr - general * ii
-            xb[0, 1, n] = not_first * ri + not_flat * ir
-            xb[1, 0, n] = general * (rr + ii) + first_deep * ri + flat * ir
-            xb[1, 1, n] = general * (ir - ri) + own_imag * ii
-            xb[2, 0, n] = first_flat * ri + pltpu.roll(first_flat * ii, 1, 0)
-            xb[2, 1, n] = zero
+            tr, ti = col_in[f, u, n], col_in[f, u, COLS + n]
+            rr, ri = turned(tr), turned(ti)
+            xb[0, 0, n] = re_r * tr + re_turned_r * rr + re_i * ti + re_turned_i * ri
+            xb[0, 1, n] = im_r * tr + im_turned_r * rr + im_i * ti + im_turned_i * ri
+            if u == 0:
+                xb[1, 0, n] = first * flat * (top * rr + bottom * ti)
+                xb[1, 1, n] = zero
 
         def group(g, carry):
             values = [(xb[g, 0, n], xb[g, 1, n]) for n in range(COLS)]
@@ -583,14 +599,17 @@
             for kc in range(COLS):
                 re, im = values[kc]
                 cs, sn = xt_ref[0, kc : kc + 1, :], xt_ref[1, kc : kc + 1, :]
-                xs[0, g, kc, :, :XB] = re * cs + im * sn
-                xs[0, g, kc, :, XB:] = im * cs - re * sn
+                xs[g, kc, :, :XB] = re * cs + im * sn
+                xs[g, kc, :, XB:] = im * cs - re * sn
             return carry
 
-        lax.fori_loop(0, 3, group, 0)
-        high, low_part = halves(xs[0].reshape(3 * COLS * SLOTS, 2 * XB))
+        lax.fori_loop(0, groups, group, 0)
+        high, low_part = halves(xs[:groups].reshape(groups * COLS * 8, 2 * XB))
         out = mm(high, wx_ref[0]) + mm(low_part, wx_ref[0]) + mm(high, wx_ref[1])
-        return out.reshape(3, COLS, SLOTS, 2 * XB)
+        return out.reshape(groups, COLS, 8, 2 * XB)
+
+    def kappa_of(u):
+        return kappa[0:2] if u == 0 else kappa[2:3]
 
     def x_derivative(re, im, sign):
         same = xt_ref[3][None, :, None, :]
@@ -599,15 +618,16 @@
             return -(re * same + im * cross), re * cross - im * same
         return re * same - im * cross, im * same + re * cross
 
-    def x_inverse(value, f):
-        high, low_part = halves(value.reshape(3 * COLS * SLOTS, 2 * XB))
+    def x_inverse(value, f, u):
+        first, groups = first_of(u), 2 - u
+        high, low_part = halves(value.reshape(groups * COLS * 8, 2 * XB))
         out = mm(high, ux_ref[0]) + mm(low_part, ux_ref[0]) + mm(high, ux_ref[1])
-        xs[0] = out.reshape(3, COLS, SLOTS, 2 * XB)
+        xs[:groups] = out.reshape(groups, COLS, 8, 2 * XB)
 
         def group(g, carry):
             values = []
             for kc in range(COLS):
-                re, im = xs[0, g, kc, :, :XB], xs[0, g, kc, :, XB:]
+                re, im = xs[g, kc, :, :XB], xs[g, kc, :, XB:]
                 cs, sn = xt_ref[0, kc : kc + 1, :], xt_ref[1, kc : kc + 1, :]
                 values.append((re * cs - im * sn, im * cs + re * sn))
             values = short_transform(values, 1.0)
@@ -616,24 +636,30 @@
                 xb[g, 1, n] = values[n][1]
             return carry
 
-        lax.fori_loop(0, 3, group, 0)
+        lax.fori_loop(0, groups, group, 0)
+        half = 0.5 * (1.0 - first) * deep
+        rest = (1.0 - first) * flat
+        lone = first * deep
+        r_re = top * half + top * flat + lone
+        r_re_turned = top * half
+        r_im, r_im_turned = -bottom * half, bottom * (half + rest)
+        i_re, i_re_turned = bottom * half, top * flat - bottom * half
+        i_im, i_im_turned = top * half + lone + bottom * rest, top * half
         for n in range(COLS):
-            lr, li = xb[0, 0, n], xb[0, 1, n]
-            hr, hi = xb[1, 0, n], xb[1, 1, n]
-            xr = xb[2, 0, n]
-            bcol_out[f, n, 0:8, :] = lr + half_general * (hr - lr)
-            bcol_out[f, n, 8:16, :] = (
-                half_general * (li - hi) + first_deep * hr + rest_flat * li + first_flat * xr
-            )
-            bcol_out[f, COLS + n, 0:8, :] = half_general * (li + hi) + first_deep * li + flat * hr
-            bcol_out[f, COLS + n, 8:16, :] = (
-                half_general * (hr - lr) + own_imag * hi + first_flat * pltpu.roll(xr, 7, 0)
-            )
+            vr, vi = xb[0, 0, n], xb[0, 1, n]
+            wr, wi = turned(vr), turned(vi)
+            out_r = r_re * vr + r_re_turned * wr + r_im * vi + r_im_turned * wi
+            out_i = i_re * vr + i_re_turned * wr + i_im * vi + i_im_turned * wi
+            if u == 0:
+                extra = first * flat * bottom
+                out_r = out_r + extra * turned(xb[1, 0, n])
+                out_i = out_i + extra * xb[1, 0, n]
+            bcol_out[f, u, n] = out_r
+            bcol_out[f, u, COLS + n] = out_i
 
     loaded(5)
     arrived("row", 0)
-    col_out[0] = row_product(fy_ref, [lines(row_in, 0)])[0].reshape(2 * COLS, 2 * SLOTS, XB)
-    send_col(0)
+    put_col(0, row_product(fy_ref, [lines(row_in, 0)])[0])
 
     for edge in y_edges():
         edge.wait_recv()
@@ -644,21 +670,25 @@
     fill_raw()
 
     loaded(6, 9)
-    arrived("col", 0)
-    spectrum = x_forward(0)
-    re, im = spectrum[..., :XB] * kappa[...], spectrum[..., XB:] * kappa[...]
-    dre, dim = x_derivative(re, im, 1)
-    x_inverse(jnp.concatenate([dre, dim], axis=-1), 0)
-    send_bcol(0)
-    x_inverse(jnp.concatenate([re, im], axis=-1), 1)
-    send_bcol(1)
+    for u in range(2):
+        arrived("col", 0, u)
+        spectrum = x_forward(0, u)
+        re, im = spectrum[..., :XB] * kappa_of(u), spectrum[..., XB:] * kappa_of(u)
+        dre, dim = x_derivative(re, im, 1)
+        x_inverse(jnp.concatenate([dre, dim], axis=-1), 0, u)
+        send_bcol(0, u)
+        if u == 1:
+            send_bcol(1, 0)
+        x_inverse(jnp.concatenate([re, im], axis=-1), 1, u)
+    send_bcol(1, 1)
 
     for edge in x_edges():
         edge.wait_recv()
     smooth()
     loaded(10, 11, 12, 13, 14)
 
-    arrived("bcol", 0)
+    arrived("bcol", 0, 0)
+    arrived("bcol", 0, 1)
     brow_out[0] = row_product(gy_ref, [lines(bcol_in, 0)])[0].reshape(ROWS, YB, XB)
     send_brow(0)
 
@@ -679,7 +709,8 @@
     send_row(1)
     writes[0].start()
 
-    arrived("bcol", 1)
+    arrived("bcol", 1, 0)
+    arrived("bcol", 1, 1)
     flow = lines(bcol_in, 1)
     plain, slope = row_product(gy_ref, [flow, y_derivative(flow, 1)])
     brow_out[1] = slope.reshape(ROWS, YB, XB)
@@ -688,8 +719,7 @@
     send_brow(2)
 
     arrived("row", 1)
-    col_out[1] = row_product(fy_ref, [lines(row_in, 1)])[0].reshape(2 * COLS, 2 * SLOTS, XB)
-    send_col(1)
+    put_col(1, row_product(fy_ref, [lines(row_in, 1)])[0])
 
     arrived("brow", 1)
 
@@ -723,22 +753,24 @@
 
     arrived("row", 2)
     arrived("row", 3)
-    across, deep = row_product(fy_ref, [lines(row_in, 2), lines(row_in, 3)])
-    summed = deep + y_derivative(across, -1)
-    col_out[2] = summed.reshape(2 * COLS, 2 * SLOTS, XB)
-    send_col(2)
-
-    arrived("col", 1)
-    flow_x = x_forward(1)
-    tre, tim = x_derivative(flow_x[..., :XB], flow_x[..., XB:], -1)
-    arrived("col", 2)
-    rest = x_forward(2)
-    tre = (tre + rest[..., :XB]) * kappa[...]
-    tim = (tim + rest[..., XB:]) * kappa[...]
-    x_inverse(jnp.concatenate([tre, tim], axis=-1), 2)
-    send_bcol(2)
-
-    arrived("bcol", 2)
+    aside, below = row_product(fy_ref, [lines(row_in, 2), lines(row_in, 3)])
+    put_col(2, below + y_derivative(aside, -1))
+
+    flows = []
+    for u in range(2):
+        arrived("col", 1, u)
+        flow_x = x_forward(1, u)
+        flows.append(x_derivative(flow_x[..., :XB], flow_x[..., XB:], -1))
+    for u in range(2):
+        arrived("col", 2, u)
+        remains = x_forward(2, u)
+        tre = (flows[u][0] + remains[..., :XB]) * kappa_of(u)
+        tim = (flows[u][1] + remains[..., XB:]) * kappa_of(u)
+        x_inverse(jnp.concatenate([tre, tim], axis=-1), 2, u)
+        send_bcol(2, u)
+
+    arrived("bcol", 2, 0)
+    arrived("bcol", 2, 1)
     brow_out[3] = row_product(gy_ref, [lines(bcol_in, 2)])[0].reshape(ROWS, YB, XB)
     send_brow(3)
 
@@ -754,9 +786,13 @@
     chunks(update_p)
     writes[3].start()
 
-    for kind, number in (("row", 4), ("col", 3), ("bcol", 3), ("brow", 4)):
-        for f in range(number):
-            all_of(kind, f).wait_send()
+    for f in range(4):
+        all_of("row", f).wait_send()
+        all_of("brow", f).wait_send()
+    for f in range(3):
+        for u in range(2):
+            all_of("col", f, u).wait_send()
+            all_of("bcol", f, u).wait_send()
     for edge in y_edges() + x_edges():
         edge.wait_send()
     for write in writes:
@@ -784,7 +820,7 @@
     wx, ux, xt = column_tables()
     brick = jax.ShapeDtypeStruct(pressure.shape, f32)
     row_buffer = lambda n: pltpu.VMEM((n, ROWS, YB, XB), f32)
-    col_buffer = lambda n: pltpu.VMEM((n, 2 * COLS, 2 * SLOTS, XB), f32)
+    col_buffer = lambda n: pltpu.VMEM((n, 2, 2 * COLS, 2 * SLOTS, XB), f32)
     results = pl.pallas_call(
         step_kernel,
         out_shape=(brick,) * 4,
@@ -793,9 +829,9 @@
         scratch_shapes=[
             row_buffer(4), row_buffer(4), col_buffer(3), col_buffer(3),
             col_buffer(3), col_buffer(3), row_buffer(4), row_buffer(4),
-            pltpu.VMEM((3, COLS, SLOTS, XB), f32),
-            pltpu.VMEM((3, 2, COLS, SLOTS, XB), f32),
-            pltpu.VMEM((1, 3, COLS, SLOTS, 2 * XB), f32),
+            pltpu.VMEM((3, COLS, 8, XB), f32),
+            pltpu.VMEM((2, 2, COLS, 8, XB), f32),
+            pltpu.VMEM((2, COLS, 8, 2 * XB), f32),
             pltpu.VMEM((2, NZ, YB, XB), f32),
             pltpu.VMEM((NZ, 2 * YB, XB), f32),
             pltpu.VMEM((2, XB, XB), f32),
@@ -811,8 +847,8 @@
             pltpu.SMEM((TAPS,), f32), pltpu.SMEM((4,), jnp.int32),
             *[pltpu.VMEM(t.shape, t.dtype) for t in (fy, gy, yd, wx, ux, xt)],
             *[pltpu.VMEM(pressure.shape, f32)] * 4,
-            pltpu.SemaphoreType.DMA((18,)),
-            pltpu.SemaphoreType.DMA((18,)),
+            pltpu.SemaphoreType.DMA((24,)),
+            pltpu.SemaphoreType.DMA((24,)),
             pltpu.SemaphoreType.DMA((15,)),
             pltpu.SemaphoreType.DMA((4,)),
         ],

time: 91.7 us -> 88.1 us (0.961)
  Pallas kernels: 91 us -> 87.3 us
    pallas_call x1, Pallas kernels: 89 us -> 85.4 us  [on_device(): pl.pallas_call(step_kernel, out_shape=(brick,) * 4, in_specs=[pl.BlockSpe...]
where the time goes in v4:
time: 88.1 us; the launch traced here: 88 us
  Pallas kernels  87.3 us (99%)
    pallas_call x1, Pallas kernels, on_device(): pl.pallas_call(step_kernel, out_shape=(brick,) * 4, in_specs=[pl.BlockSpe...  85.4 us
    pallas_call x1, Pallas kernels, on_device(): pl.pallas_call(write_kernel, out_shape=(brick,) * 4, in_specs=[pl.BlockSp...  1.98 us

profile of v4, /device:TPU:1, one launch (start us, length us, event | category | flops | bytes accessed | tf_op | source)
XLA Modules:
  0.0 88.0 jit_solution(3228037776433686537)
XLA Ops:
  0.6 85.4 %shard_map.174 = (f32[16,32,128]{2,1,0:T(8,128)}, f32[16,32,128]{2,1,0:T(8,128)}, f32[16,32,128]{2,1,0:T(8,128)}, f32[16,32,128]{2,1,0:T(8,128)}) custom-call(s32[16,32,128]{2,1,0:T(8,128)} %lab_hbm.1, f32[16,32,128]{2,1,0:T(8,128)} %p_hbm.1, f32[16,32,128]{2,1,0:T(8,128)} %vx_hbm.1, f32[16,32,128]{2,1,0:T(8,128)} %vy_hbm.1, f32[16,32,128]{2,1,0:T(8,128)} %vz_hbm.1, ...), custom_call_target="tpu_custom_call" | custom-call | tf_op jit(solution)/shard_map/pallas_call | solution.py:824
  86.0 2.0 %shard_map.175 = (f32[16,32,128]{2,1,0:T(8,128)}, f32[16,32,128]{2,1,0:T(8,128)}, f32[16,32,128]{2,1,0:T(8,128)}, f32[16,32,128]{2,1,0:T(8,128)}) custom-call(f32[16,32,128]{2,1,0:T(8,128)} %get-tuple-element.8.a, f32[16,32,128]{2,1,0:T(8,128)} %get-tuple-element.9.b, f32[16,32,128]{2,1,0:T(8,128)} %get-tuple-element.10.c, f32[16,32,128]{2,1,0:T(8,128)} %get-tuple-element.11.d), custom_call_target="tpu_custom_call" | custom-call | tf_op jit(solution)/shard_map/pallas_call | solution.py:864

commit v5 on v4

--- a/solution.py
+++ b/solution.py
@@ -19,7 +19,7 @@
 YB, XB = NY // ROWS, NX // COLS
 SLOTS, HALO = 4, 16
 CHUNK = 2 * COLS * SLOTS
-VMEM_BYTES = 67043328
+STEP_BYTES, WRITE_BYTES = 40 << 20, 4 << 20
 TAPS, LABELS = 33, 12
 f32, bf16 = jnp.float32, jnp.bfloat16
 
@@ -206,21 +206,13 @@
 def step_kernel(
     lab_hbm, p_hbm, vx_hbm, vy_hbm, vz_hbm, speed_hbm, density_hbm, taps_hbm, width_hbm,
     fy_hbm, gy_hbm, yd_hbm, wx_hbm, ux_hbm, xt_hbm,
-    po_hbm, vxo_hbm, vyo_hbm, vzo_hbm,
+    po_ref, vxo_ref, vyo_ref, vzo_ref,
     row_out, row_in, col_out, col_in, bcol_out, bcol_in, brow_out, brow_in,
     kappa, xb, xs, coef, lab, edge_out, edge_in, raw, across, edge_band, down, damp,
     lab_ref, p_ref, vx_ref, vy_ref, vz_ref, speed_ref, density_ref, taps_ref, width_ref,
     fy_ref, gy_ref, yd_ref, wx_ref, ux_ref, xt_ref,
-    po_ref, vxo_ref, vyo_ref, vzo_ref,
-    send_sem, recv_sem, load_sem, store_sem,
+    send_sem, recv_sem, load_sem,
 ):
-    writes = [
-        pltpu.make_async_copy(source, target, store_sem.at[n])
-        for n, (source, target) in enumerate(
-            [(vxo_ref, vxo_hbm), (vyo_ref, vyo_hbm), (vzo_ref, vzo_hbm), (po_ref, po_hbm)]
-        )
-    ]
-
     def loaded(*numbers):
         for n in numbers:
             fetches[n].wait()
@@ -707,7 +699,6 @@
 
     chunks(update_x)
     send_row(1)
-    writes[0].start()
 
     arrived("bcol", 1, 0)
     arrived("bcol", 1, 1)
@@ -735,7 +726,6 @@
 
     chunks(update_y)
     send_row(2)
-    writes[1].start()
 
     arrived("brow", 2)
 
@@ -749,7 +739,6 @@
 
     chunks(update_z)
     send_row(3)
-    writes[2].start()
 
     arrived("row", 2)
     arrived("row", 3)
@@ -784,7 +773,6 @@
             po_ref[z, rows, :] = both * (both * p_ref[z, rows, :] - change)
 
     chunks(update_p)
-    writes[3].start()
 
     for f in range(4):
         all_of("row", f).wait_send()
@@ -795,21 +783,15 @@
             all_of("bcol", f, u).wait_send()
     for edge in y_edges() + x_edges():
         edge.wait_send()
-    for write in writes:
-        write.wait()
-
-
-def write_kernel(a, b, c, d, a_out, b_out, c_out, d_out, held, in_sem, out_sem):
-    arrays = ((a, a_out), (b, b_out), (c, c_out), (d, d_out))
-    loads = [pltpu.make_async_copy(x, held.at[n], in_sem.at[n]) for n, (x, _) in enumerate(arrays)]
-    stores = [pltpu.make_async_copy(held.at[n], y, out_sem.at[n]) for n, (_, y) in enumerate(arrays)]
-    for load in loads:
-        load.start()
-    for load, store in zip(loads, stores):
-        load.wait()
-        store.start()
-    for store in stores:
-        store.wait()
+
+
+def write_kernel(a, b, c, d, a_out, b_out, c_out, d_out, sem):
+    pairs = ((a, a_out), (b, b_out), (c, c_out), (d, d_out))
+    copies = [pltpu.make_async_copy(x, y, sem.at[n]) for n, (x, y) in enumerate(pairs)]
+    for copy in copies:
+        copy.start()
+    for copy in copies:
+        copy.wait()
 
 
 def on_device(
@@ -821,11 +803,12 @@
     brick = jax.ShapeDtypeStruct(pressure.shape, f32)
     row_buffer = lambda n: pltpu.VMEM((n, ROWS, YB, XB), f32)
     col_buffer = lambda n: pltpu.VMEM((n, 2, 2 * COLS, 2 * SLOTS, XB), f32)
+    hold = lambda t: pltpu.with_memory_space_constraint(t, pltpu.HBM)
     results = pl.pallas_call(
         step_kernel,
         out_shape=(brick,) * 4,
         in_specs=[pl.BlockSpec(memory_space=pl.ANY)] * 15,
-        out_specs=(pl.BlockSpec(memory_space=pl.ANY),) * 4,
+        out_specs=(pl.BlockSpec(memory_space=pltpu.VMEM),) * 4,
         scratch_shapes=[
             row_buffer(4), row_buffer(4), col_buffer(3), col_buffer(3),
             col_buffer(3), col_buffer(3), row_buffer(4), row_buffer(4),
@@ -846,31 +829,31 @@
             pltpu.SMEM((LABELS,), f32), pltpu.SMEM((LABELS,), f32),
             pltpu.SMEM((TAPS,), f32), pltpu.SMEM((4,), jnp.int32),
             *[pltpu.VMEM(t.shape, t.dtype) for t in (fy, gy, yd, wx, ux, xt)],
-            *[pltpu.VMEM(pressure.shape, f32)] * 4,
             pltpu.SemaphoreType.DMA((24,)),
             pltpu.SemaphoreType.DMA((24,)),
             pltpu.SemaphoreType.DMA((15,)),
-            pltpu.SemaphoreType.DMA((4,)),
         ],
         compiler_params=pltpu.CompilerParams(
-            collective_id=0, has_side_effects=True, vmem_limit_bytes=VMEM_BYTES
+            collective_id=0, has_side_effects=True, vmem_limit_bytes=STEP_BYTES
         ),
     )(
-        labels, pressure, velocity_x, velocity_y, velocity_z,
-        speed_table, density_table, filter_taps, layer_width,
-        jnp.asarray(fy), jnp.asarray(gy), jnp.asarray(yd),
-        jnp.asarray(wx), jnp.asarray(ux), jnp.asarray(xt),
+        *[
+            hold(t)
+            for t in (
+                labels, pressure, velocity_x, velocity_y, velocity_z,
+                speed_table, density_table, filter_taps, layer_width,
+                jnp.asarray(fy), jnp.asarray(gy), jnp.asarray(yd),
+                jnp.asarray(wx), jnp.asarray(ux), jnp.asarray(xt),
+            )
+        ]
     )
     return pl.pallas_call(
         write_kernel,
         out_shape=(brick,) * 4,
-        in_specs=[pl.BlockSpec(memory_space=pl.ANY)] * 4,
+        in_specs=[pl.BlockSpec(memory_space=pltpu.VMEM)] * 4,
         out_specs=(pl.BlockSpec(memory_space=pl.ANY),) * 4,
-        scratch_shapes=[
-            pltpu.VMEM((4,) + pressure.shape, f32),
-            pltpu.SemaphoreType.DMA((4,)), pltpu.SemaphoreType.DMA((4,)),
-        ],
-        compiler_params=pltpu.CompilerParams(vmem_limit_bytes=VMEM_BYTES),
+        scratch_shapes=[pltpu.SemaphoreType.DMA((4,))],
+        compiler_params=pltpu.CompilerParams(vmem_limit_bytes=WRITE_BYTES),
     )(*results)
 
 

time: 88.1 us -> 86.5 us (0.982)
  Pallas kernels: 87.3 us -> 85.7 us
    pallas_call x1, Pallas kernels: 1.98 us -> 1 us  [on_device(): pl.pallas_call(write_kernel, out_shape=(brick,) * 4, in_specs=[pl.BlockSp...]
where the time goes in v5:
time: 86.5 us; the launch traced here: 86.4 us
  Pallas kernels  85.7 us (99%)
    pallas_call x1, Pallas kernels, on_device(): pl.pallas_call(step_kernel, out_shape=(brick,) * 4, in_specs=[pl.BlockSpe...  84.7 us

profile of v5, /device:TPU:1, one launch (start us, length us, event | category | flops | bytes accessed | tf_op | source)
XLA Modules:
  0.0 86.4 jit_solution(13947465250482597576)
XLA Ops:
  0.6 84.7 %shard_map.174 = (f32[16,32,128]{2,1,0:T(8,128)S(1)}, f32[16,32,128]{2,1,0:T(8,128)S(1)}, f32[16,32,128]{2,1,0:T(8,128)S(1)}, f32[16,32,128]{2,1,0:T(8,128)S(1)}) custom-call(s32[16,32,128]{2,1,0:T(8,128)} %lab_hbm.1, f32[16,32,128]{2,1,0:T(8,128)} %p_hbm.1, f32[16,32,128]{2,1,0:T(8,128)} %vx_hbm.1, f32[16,32,128]{2,1,0:T(8,128)} %vy_hbm.1, ...), custom_call_target="tpu_custom_call" | custom-call | tf_op jit(solution)/shard_map/pallas_call | solution.py:807
  85.4 1.0 %shard_map.175 = (f32[16,32,128]{2,1,0:T(8,128)}, f32[16,32,128]{2,1,0:T(8,128)}, f32[16,32,128]{2,1,0:T(8,128)}, f32[16,32,128]{2,1,0:T(8,128)}) custom-call(f32[16,32,128]{2,1,0:T(8,128)S(1)} %get-tuple-element.8.a, f32[16,32,128]{2,1,0:T(8,128)S(1)} %get-tuple-element.9.b, f32[16,32,128]{2,1,0:T(8,128)S(1)} %get-tuple-element.10.c, ...), custom_call_target="tpu_custom_call" | custom-call | tf_op jit(solution)/shard_map/pallas_call | solution.py:850

commit v6 on v5

--- a/solution.py
+++ b/solution.py
@@ -44,14 +44,7 @@
     forward = order(real, imag).reshape(NY, NY)
     weight = np.where(slot == 0, 1.0, 2.0)[:, None] / NY
     inverse = order(real * weight, imag * weight).reshape(NY, NY).T
-    wave = 2.0 * np.pi * slot / NY
-    same = -wave * np.sin(0.5 * wave)
-    cross = wave * np.cos(0.5 * wave)
-    same_imag = same.copy()
-    same_imag[0] = -np.pi
-    tables = [order(same, same_imag), order(-cross, cross)]
-    wide = [np.broadcast_to(t.reshape(-1, 2 * SLOTS, 1), (NY // 8, 8, XB)) for t in tables]
-    return split_table(forward), split_table(inverse), np.stack(wide).astype(np.float32)
+    return split_table(forward), split_table(inverse)
 
 
 def column_tables():
@@ -205,12 +198,12 @@
 
 def step_kernel(
     lab_hbm, p_hbm, vx_hbm, vy_hbm, vz_hbm, speed_hbm, density_hbm, taps_hbm, width_hbm,
-    fy_hbm, gy_hbm, yd_hbm, wx_hbm, ux_hbm, xt_hbm,
+    fy_hbm, gy_hbm, wx_hbm, ux_hbm, xt_hbm,
     po_ref, vxo_ref, vyo_ref, vzo_ref,
     row_out, row_in, col_out, col_in, bcol_out, bcol_in, brow_out, brow_in,
     kappa, xb, xs, coef, lab, edge_out, edge_in, raw, across, edge_band, down, damp,
     lab_ref, p_ref, vx_ref, vy_ref, vz_ref, speed_ref, density_ref, taps_ref, width_ref,
-    fy_ref, gy_ref, yd_ref, wx_ref, ux_ref, xt_ref,
+    fy_ref, gy_ref, wx_ref, ux_ref, xt_ref, yd_ref,
     send_sem, recv_sem, load_sem,
 ):
     def loaded(*numbers):
@@ -270,7 +263,7 @@
                 (p_hbm, p_ref), (lab_hbm, lab_ref), (xt_hbm, xt_ref), (taps_hbm, taps_ref),
                 (width_hbm, width_ref), (fy_hbm, fy_ref), (wx_hbm, wx_ref),
                 (speed_hbm, speed_ref), (density_hbm, density_ref), (ux_hbm, ux_ref),
-                (gy_hbm, gy_ref), (vx_hbm, vx_ref), (yd_hbm, yd_ref), (vy_hbm, vy_ref),
+                (gy_hbm, gy_ref), (vx_hbm, vx_ref), (vy_hbm, vy_ref),
                 (vz_hbm, vz_ref),
             ]
         )
@@ -561,6 +554,21 @@
         result = mm(table[0], high) + mm(table[0], low_part) + mm(table[1], high)
         return [result[:, :XB], result[:, XB:]]
 
+    def fill_slopes(n, carry):
+        slots = n * SLOTS + tile_rows % SLOTS
+        angle = slots.astype(f32) * np.float32(math.pi / NY)
+        square = angle * angle
+        sine, cosine = one, one
+        for k in range(6, 0, -1):
+            sine = 1.0 - square * np.float32(1.0 / (2 * k * (2 * k + 1))) * sine
+        for k in range(7, 0, -1):
+            cosine = 1.0 - square * np.float32(1.0 / (2 * k * (2 * k - 1))) * cosine
+        same = -2.0 * square * sine
+        edge = jnp.where(slots == 0, bottom * np.float32(math.pi), zero)
+        yd_ref[0, n] = same - edge
+        yd_ref[1, n] = 2.0 * angle * cosine * (bottom - top)
+        return carry
+
     def y_derivative(value, sign):
         tiles = value.reshape(NY // 8, 8, XB)
         same = tiles * yd_ref[0]
@@ -660,33 +668,30 @@
         edge.start()
     loaded(7, 8)
     fill_raw()
+    lax.fori_loop(0, NY // 8, fill_slopes, 0)
 
     loaded(6, 9)
     for u in range(2):
         arrived("col", 0, u)
         spectrum = x_forward(0, u)
         re, im = spectrum[..., :XB] * kappa_of(u), spectrum[..., XB:] * kappa_of(u)
+        x_inverse(jnp.concatenate([re, im], axis=-1), 1, u)
+        send_bcol(1, u)
+        if u == 1:
+            send_bcol(0, 0)
         dre, dim = x_derivative(re, im, 1)
         x_inverse(jnp.concatenate([dre, dim], axis=-1), 0, u)
-        send_bcol(0, u)
-        if u == 1:
-            send_bcol(1, 0)
-        x_inverse(jnp.concatenate([re, im], axis=-1), 1, u)
-    send_bcol(1, 1)
+    send_bcol(0, 1)
 
     for edge in x_edges():
         edge.wait_recv()
     smooth()
-    loaded(10, 11, 12, 13, 14)
-
-    arrived("bcol", 0, 0)
-    arrived("bcol", 0, 1)
-    brow_out[0] = row_product(gy_ref, [lines(bcol_in, 0)])[0].reshape(ROWS, YB, XB)
-    send_brow(0)
+    loaded(10, 11, 12, 13)
 
     dx = damp[0:8]
 
-    arrived("brow", 0)
+    def rows_of_y(rows):
+        return damp[pl.ds(pl.multiple_of(rows.start + 8, 8), 8), :]
 
     def update_x(rows):
         grad = depth_inverse(load(brow_in.at[0], rows))
@@ -697,8 +702,23 @@
         store(vxo_ref, rows, fresh)
         store(row_out.at[1], rows, depth_forward(fresh))
 
-    chunks(update_x)
-    send_row(1)
+    def update_y(rows):
+        grad = depth_inverse(load(brow_in.at[1], rows))
+        dy = rows_of_y(rows)
+        fresh = []
+        for z in range(NZ):
+            change = time_step * coef[0, z, rows, :] * grad[z]
+            fresh.append(dy * (dy * vy_ref[z, rows, :] - change))
+        store(vyo_ref, rows, fresh)
+        store(row_out.at[2], rows, depth_forward(fresh))
+
+    def update_z(rows):
+        grad = depth_inverse(depth_derivative(load(brow_in.at[2], rows), 1))
+        fresh = []
+        for z in range(NZ):
+            fresh.append(vz_ref[z, rows, :] - time_step * coef[0, z, rows, :] * grad[z])
+        store(vzo_ref, rows, fresh)
+        store(row_out.at[3], rows, depth_derivative(depth_forward(fresh), -1))
 
     arrived("bcol", 1, 0)
     arrived("bcol", 1, 1)
@@ -709,52 +729,38 @@
     brow_out[2] = plain.reshape(ROWS, YB, XB)
     send_brow(2)
 
+    arrived("bcol", 0, 0)
+    arrived("bcol", 0, 1)
+    brow_out[0] = row_product(gy_ref, [lines(bcol_in, 0)])[0].reshape(ROWS, YB, XB)
+    send_brow(0)
+
+    arrived("brow", 1)
+    chunks(update_y)
+    send_row(2)
+    arrived("brow", 2)
+    chunks(update_z)
+    send_row(3)
+    arrived("brow", 0)
+    chunks(update_x)
+    send_row(1)
+
+    arrived("row", 2)
+    aside = y_derivative(row_product(fy_ref, [lines(row_in, 2)])[0], -1)
+    arrived("row", 3)
+    put_col(2, aside + row_product(fy_ref, [lines(row_in, 3)])[0])
     arrived("row", 1)
     put_col(1, row_product(fy_ref, [lines(row_in, 1)])[0])
 
-    arrived("brow", 1)
-
-    def update_y(rows):
-        grad = depth_inverse(load(brow_in.at[1], rows))
-        dy = damp[pl.ds(pl.multiple_of(rows.start + 8, 8), 8), :]
-        fresh = []
-        for z in range(NZ):
-            change = time_step * coef[0, z, rows, :] * grad[z]
-            fresh.append(dy * (dy * vy_ref[z, rows, :] - change))
-        store(vyo_ref, rows, fresh)
-        store(row_out.at[2], rows, depth_forward(fresh))
-
-    chunks(update_y)
-    send_row(2)
-
-    arrived("brow", 2)
-
-    def update_z(rows):
-        grad = depth_inverse(depth_derivative(load(brow_in.at[2], rows), 1))
-        fresh = []
-        for z in range(NZ):
-            fresh.append(vz_ref[z, rows, :] - time_step * coef[0, z, rows, :] * grad[z])
-        store(vzo_ref, rows, fresh)
-        store(row_out.at[3], rows, depth_derivative(depth_forward(fresh), -1))
-
-    chunks(update_z)
-    send_row(3)
-
-    arrived("row", 2)
-    arrived("row", 3)
-    aside, below = row_product(fy_ref, [lines(row_in, 2), lines(row_in, 3)])
-    put_col(2, below + y_derivative(aside, -1))
-
-    flows = []
+    remains = []
+    for u in range(2):
+        arrived("col", 2, u)
+        remains.append(x_forward(2, u))
     for u in range(2):
         arrived("col", 1, u)
         flow_x = x_forward(1, u)
-        flows.append(x_derivative(flow_x[..., :XB], flow_x[..., XB:], -1))
-    for u in range(2):
-        arrived("col", 2, u)
-        remains = x_forward(2, u)
-        tre = (flows[u][0] + remains[..., :XB]) * kappa_of(u)
-        tim = (flows[u][1] + remains[..., XB:]) * kappa_of(u)
+        tre, tim = x_derivative(flow_x[..., :XB], flow_x[..., XB:], -1)
+        tre = (tre + remains[u][..., :XB]) * kappa_of(u)
+        tim = (tim + remains[u][..., XB:]) * kappa_of(u)
         x_inverse(jnp.concatenate([tre, tim], axis=-1), 2, u)
         send_bcol(2, u)
 
@@ -798,7 +804,7 @@
     labels, pressure, velocity_x, velocity_y, velocity_z,
     speed_table, density_table, filter_taps, layer_width,
 ):
-    fy, gy, yd = row_tables()
+    fy, gy = row_tables()
     wx, ux, xt = column_tables()
     brick = jax.ShapeDtypeStruct(pressure.shape, f32)
     row_buffer = lambda n: pltpu.VMEM((n, ROWS, YB, XB), f32)
@@ -807,7 +813,7 @@
     results = pl.pallas_call(
         step_kernel,
         out_shape=(brick,) * 4,
-        in_specs=[pl.BlockSpec(memory_space=pl.ANY)] * 15,
+        in_specs=[pl.BlockSpec(memory_space=pl.ANY)] * 14,
         out_specs=(pl.BlockSpec(memory_space=pltpu.VMEM),) * 4,
         scratch_shapes=[
             row_buffer(4), row_buffer(4), col_buffer(3), col_buffer(3),
@@ -828,10 +834,11 @@
             *[pltpu.VMEM(pressure.shape, f32)] * 4,
             pltpu.SMEM((LABELS,), f32), pltpu.SMEM((LABELS,), f32),
             pltpu.SMEM((TAPS,), f32), pltpu.SMEM((4,), jnp.int32),
-            *[pltpu.VMEM(t.shape, t.dtype) for t in (fy, gy, yd, wx, ux, xt)],
+            *[pltpu.VMEM(t.shape, t.dtype) for t in (fy, gy, wx, ux, xt)],
+            pltpu.VMEM((2, NY // 8, 8, XB), f32),
             pltpu.SemaphoreType.DMA((24,)),
             pltpu.SemaphoreType.DMA((24,)),
-            pltpu.SemaphoreType.DMA((15,)),
+            pltpu.SemaphoreType.DMA((14,)),
         ],
         compiler_params=pltpu.CompilerParams(
             collective_id=0, has_side_effects=True, vmem_limit_bytes=STEP_BYTES
@@ -842,7 +849,7 @@
             for t in (
                 labels, pressure, velocity_x, velocity_y, velocity_z,
                 speed_table, density_table, filter_taps, layer_width,
-                jnp.asarray(fy), jnp.asarray(gy), jnp.asarray(yd),
+                jnp.asarray(fy), jnp.asarray(gy),
                 jnp.asarray(wx), jnp.asarray(ux), jnp.asarray(xt),
             )
         ]

time: 86.5 us -> 84.3 us (0.975)
  Pallas kernels: 85.7 us -> 83.6 us
    pallas_call x1, Pallas kernels: 84.7 us -> 82.6 us  [on_device(): pl.pallas_call(step_kernel, out_shape=(brick,) * 4, in_specs=[pl.BlockSpe...]
where the time goes in v6:
time: 84.3 us; the launch traced here: 84.2 us
  Pallas kernels  83.6 us (99%)
    pallas_call x1, Pallas kernels, on_device(): pl.pallas_call(step_kernel, out_shape=(brick,) * 4, in_specs=[pl.BlockSpe...  82.6 us

profile of v6, /device:TPU:1, one launch (start us, length us, event | category | flops | bytes accessed | tf_op | source)
XLA Modules:
  0.0 84.2 jit_solution(3289446005118976767)
XLA Ops:
  0.6 82.6 %shard_map.165 = (f32[16,32,128]{2,1,0:T(8,128)S(1)}, f32[16,32,128]{2,1,0:T(8,128)S(1)}, f32[16,32,128]{2,1,0:T(8,128)S(1)}, f32[16,32,128]{2,1,0:T(8,128)S(1)}) custom-call(s32[16,32,128]{2,1,0:T(8,128)} %lab_hbm.1, f32[16,32,128]{2,1,0:T(8,128)} %p_hbm.1, f32[16,32,128]{2,1,0:T(8,128)} %vx_hbm.1, f32[16,32,128]{2,1,0:T(8,128)} %vy_hbm.1, ...), custom_call_target="tpu_custom_call" | custom-call | tf_op jit(solution)/shard_map/pallas_call | solution.py:813
  83.2 1.0 %shard_map.166 = (f32[16,32,128]{2,1,0:T(8,128)}, f32[16,32,128]{2,1,0:T(8,128)}, f32[16,32,128]{2,1,0:T(8,128)}, f32[16,32,128]{2,1,0:T(8,128)}) custom-call(f32[16,32,128]{2,1,0:T(8,128)S(1)} %get-tuple-element.8.a, f32[16,32,128]{2,1,0:T(8,128)S(1)} %get-tuple-element.9.b, f32[16,32,128]{2,1,0:T(8,128)S(1)} %get-tuple-element.10.c, ...), custom_call_target="tpu_custom_call" | custom-call | tf_op jit(solution)/shard_map/pallas_call | solution.py:857

commit v7 on v6

--- a/solution.py
+++ b/solution.py
@@ -537,10 +537,15 @@
     def lines(ref, f):
         return ref[f].reshape(NY, XB)
 
-    def put_col(f, value):
-        col_out[f] = value.reshape(2, 2 * COLS, 2 * SLOTS, XB)
-        send_col(f, 0)
-        send_col(f, 1)
+    def put_col(f, values, add=None):
+        span = NY // 2
+        for u in range(2):
+            rows = slice(u * span, (u + 1) * span)
+            out = row_product(fy_ref[:, rows, :], [values])[0]
+            if add is not None:
+                out = out + add[rows]
+            col_out[f, u] = out.reshape(2 * COLS, 2 * SLOTS, XB)
+            send_col(f, u)
 
     def row_product(table, values):
         parts = [halves(v) for v in values]
@@ -659,7 +664,7 @@
 
     loaded(5)
     arrived("row", 0)
-    put_col(0, row_product(fy_ref, [lines(row_in, 0)])[0])
+    put_col(0, lines(row_in, 0))
 
     for edge in y_edges():
         edge.wait_recv()
@@ -747,9 +752,9 @@
     arrived("row", 2)
     aside = y_derivative(row_product(fy_ref, [lines(row_in, 2)])[0], -1)
     arrived("row", 3)
-    put_col(2, aside + row_product(fy_ref, [lines(row_in, 3)])[0])
+    put_col(2, lines(row_in, 3), aside)
     arrived("row", 1)
-    put_col(1, row_product(fy_ref, [lines(row_in, 1)])[0])
+    put_col(1, lines(row_in, 1))
 
     remains = []
     for u in range(2):

time: 84.3 us -> 84 us (level)
  no operation moved by 1% of the time
where the time goes in v7:
time: 84 us
  Pallas kernels  83.3 us (99%)
    pallas_call x1, Pallas kernels, on_device(): pl.pallas_call(step_kernel, out_shape=(brick,) * 4, in_specs=[pl.BlockSpe...  82.3 us

profile of v7, /device:TPU:1, one launch (start us, length us, event | category | flops | bytes accessed | tf_op | source)
XLA Modules:
  0.0 84.0 jit_solution(11246003645785200068)
XLA Ops:
  0.6 82.3 %shard_map.165 = (f32[16,32,128]{2,1,0:T(8,128)S(1)}, f32[16,32,128]{2,1,0:T(8,128)S(1)}, f32[16,32,128]{2,1,0:T(8,128)S(1)}, f32[16,32,128]{2,1,0:T(8,128)S(1)}) custom-call(s32[16,32,128]{2,1,0:T(8,128)} %lab_hbm.1, f32[16,32,128]{2,1,0:T(8,128)} %p_hbm.1, f32[16,32,128]{2,1,0:T(8,128)} %vx_hbm.1, f32[16,32,128]{2,1,0:T(8,128)} %vy_hbm.1, ...), custom_call_target="tpu_custom_call" | custom-call | tf_op jit(solution)/shard_map/pallas_call | solution.py:818
  83.0 1.0 %shard_map.166 = (f32[16,32,128]{2,1,0:T(8,128)}, f32[16,32,128]{2,1,0:T(8,128)}, f32[16,32,128]{2,1,0:T(8,128)}, f32[16,32,128]{2,1,0:T(8,128)}) custom-call(f32[16,32,128]{2,1,0:T(8,128)S(1)} %get-tuple-element.8.a, f32[16,32,128]{2,1,0:T(8,128)S(1)} %get-tuple-element.9.b, f32[16,32,128]{2,1,0:T(8,128)S(1)} %get-tuple-element.10.c, ...), custom_call_target="tpu_custom_call" | custom-call | tf_op jit(solution)/shard_map/pallas_call | solution.py:862
